TPU v7x, 8 devices: a whole 2x2x1 slice. The times are simulated.
8 devices in a mesh: spin: 1 (over z), row: 2 (over y), col: 4 (over x, core).
Axes of the slice: x: 2, y: 2, z: 1, core: 2. Of those that a mesh axis runs over, the one named last changes fastest.
Arguments:
- hamiltonian: float32 [2048, 2048], P(('spin', 'row'), 'col')
- bounds: float32 [2], P('spin')
- n_occ: int32 [1], P('spin')
Outputs:
- output 1: float32 [2048, 2048], P(('spin', 'row'), 'col')
- output 2: float32 [1], P('spin')
All inputs are finite; a program needn't handle non-finite values.
Results may differ from a plain program's by a relative error of at most 0.001.
Values sent between devices are 32-bit elements.
A program may use at most 1 GiB of HBM per device.

v0:
```python
import jax
import jax.numpy as jnp
from jax import lax
from jax.sharding import PartitionSpec as P

STEPS = 3


def solution(mesh):
    n_cols = mesh.shape["col"]
    highest = lax.Precision.HIGHEST

    def local_fn(ham_blk, bounds, n_occ):
        rows_n, cols_n = ham_blk.shape
        mat_order = cols_n * n_cols
        row_ids = lax.axis_index("row") * rows_n + lax.broadcasted_iota(jnp.int32, (rows_n, 1), 0)
        col_ids = lax.axis_index("col") * cols_n + lax.broadcasted_iota(jnp.int32, (1, cols_n), 1)
        diag_mask = row_ids == col_ids
        occupied = n_occ[0].astype(jnp.float32)
        mu_val = lax.psum(jnp.sum(jnp.where(diag_mask, ham_blk, 0.0)), ("row", "col")) / mat_order
        lam_scale = jnp.minimum(occupied / (bounds[1] - mu_val), (mat_order - occupied) / (mu_val - bounds[0]))
        density = jnp.where(diag_mask, (lam_scale * mu_val + occupied) / mat_order, 0.0) - (lam_scale / mat_order) * ham_blk
        for _ in range(STEPS):
            x_rows = lax.all_gather(density, "col", axis=1, tiled=True)
            x_cols = lax.all_gather(density, "row", axis=0, tiled=True)
            dens_sq = jnp.dot(x_rows, x_cols, precision=highest, preferred_element_type=jnp.float32)
            sq_rows = lax.all_gather(dens_sq, "col", axis=1, tiled=True)
            dens_cube = jnp.dot(sq_rows, x_cols, precision=highest, preferred_element_type=jnp.float32)
            part_sums = jnp.stack([jnp.sum(jnp.where(diag_mask, density, 0.0)), jnp.sum(density * density), jnp.sum(dens_sq * density)])
            traces = lax.psum(part_sums, ("row", "col"))
            mix_coef = (traces[1] - traces[2]) / (traces[0] - traces[1])
            density = ((1.0 - 2.0 * mix_coef) * density + (1.0 + mix_coef) * dens_sq - dens_cube) / (1.0 - mix_coef)
        energy = 2.0 * lax.psum(jnp.sum(density * ham_blk), ("row", "col"))
        return density, energy[None]

    spec_mat = P(("spin", "row"), "col")
    return jax.shard_map(local_fn, mesh=mesh, in_specs=(spec_mat, P("spin"), P("spin")), out_specs=(spec_mat, P("spin")), check_vma=False)
```

profile of v0, /device:TPU:0, one launch (start us, length us, event | category | flops | bytes accessed | tf_op | source)
XLA Modules:
  0.0 693.5 jit_solution(14283955586171789999)
XLA Ops:
  7.2 0.0 copy-start.3
  7.2 0.0 copy-start.4
  7.2 0.0 all-gather.12.cloned.1.call-start
  7.3 2.9 fusion
  10.2 25.3 %psum.35 = f32[]{:T(128)} all-reduce(f32[]{:T(128)} %fusion), channel_id=1, replica_groups=mesh['spin'=1,'row'=2,'col'=4] {'row','col'}, use_global_device_ids=true, to_apply=%region_1.2 | all-reduce | flops 1 | bytes 8 | tf_op jit(solution)/shard_map/psum | solution.py:20
  35.5 0.0 copy-done.4
  35.5 0.7 fusion.8
  38.8 0.0 copy-done.3
  38.8 1.6 fusion.1
  40.4 0.0 copy-start.1
  40.4 0.0 all-gather.12.cloned.1.call-update
  40.4 0.0 all-gather.10.cloned.1.call-start
  40.5 0.7 all-gather.10.cloned.1.call-update
  41.2 0.0 all-gather.14.cloned.1.call-start
  41.2 54.5 %all-gather.12.cloned.1.call-done = f32[2048,512]{1,0:T(8,128)} async-done(((f32[1024,512]{1,0:T(8,128)}), f32[2048,512]{1,0:T(8,128)}) %all-gather.12.cloned.1.call-update) | async-done | bytes 4194320 | tf_op jit(solution)/shard_map/all_gather | solution.py:25
  95.8 57.9 %all-gather.10.cloned.1.call-done = f32[1024,2048]{1,0:T(8,128)} async-done(((f32[1024,512]{1,0:T(8,128)}), f32[1024,2048]{1,0:T(8,128)}) %all-gather.10.cloned.1.call-update) | async-done | bytes 8388624 | tf_op jit(solution)/shard_map/all_gather | solution.py:24
  153.6 0.0 copy-done.1
  153.6 19.1 %fusion.2 = (f32[]{:T(128)}, f32[]{:T(128)}, f32[]{:T(128)}, f32[1024,512]{1,0:T(8,128)}) fusion(f32[1024,512]{1,0:T(8,128)S(1)} %copy-done.1, s32[512]{0:T(512)S(1)} %iota_add_fusion.1, s32[1024]{0:T(1024)S(1)} %iota_add_fusion, f32[1024,2048]{1,0:T(8,128)} %all-gather.10.cloned.1.call-done, f32[2048,512]{1,0:T(8,128)} %all-gather.12.cloned.1.call-done), kind=kOutput, calls=%fused_computation.7 | convolution fusion | flops 12888571904 | bytes 16783372 | tf_op jit(solution)/shard_map/dot_general | solution.py:26
  172.7 0.0 all-gather.14.cloned.1.call-update
  172.7 0.0 all-gather.18.cloned.1.call-start
  172.8 2.0 pad_maximum_fusion
  174.8 22.8 %psum.36 = f32[3]{0:T(128)S(1)} all-reduce(f32[3]{0:T(128)S(1)} %pad_maximum_fusion), channel_id=1, replica_groups=mesh['spin'=1,'row'=2,'col'=4] {'row','col'}, use_global_device_ids=true, to_apply=%region_5.6 | all-reduce | flops 3 | bytes 24 | tf_op jit(solution)/shard_map/psum | solution.py:30
  197.6 0.7 fusion.7
  200.9 28.6 %all-gather.14.cloned.1.call-done = f32[1024,2048]{1,0:T(8,128)} async-done(((f32[1024,512]{1,0:T(8,128)}), f32[1024,2048]{1,0:T(8,128)}) %all-gather.14.cloned.1.call-update) | async-done | bytes 8388624 | tf_op jit(solution)/shard_map/all_gather | solution.py:27
  229.5 18.5 %subtract_divide_fusion.2 = f32[1024,512]{1,0:T(8,128)} fusion(f32[1024,512]{1,0:T(8,128)} %get-tuple-element.22, f32[1024,512]{1,0:T(8,128)S(1)} %copy-done.1, f32[1024,2048]{1,0:T(8,128)} %all-gather.14.cloned.1.call-done, f32[2048,512]{1,0:T(8,128)} %all-gather.12.cloned.1.call-done, f32[]{:T(128)} %bitcast.8, f32[]{:T(128)} %bitcast.7, f32[]{:T(128)} %bitcast.6), kind=kOutput, calls=%fused_computation.17 | convolution fusion | flops 12887523328 | bytes 18874380 | tf_op jit(solution)/shard_map/dot_general | solution.py:28
  248.0 0.0 copy-start.2
  248.0 0.0 all-gather.18.cloned.1.call-update
  248.0 0.0 all-gather.16.cloned.1.call-start
  248.1 0.5 all-gather.16.cloned.1.call-update
  248.6 0.2 all-gather.20.cloned.1.call-start
  248.8 53.7 %all-gather.18.cloned.1.call-done = f32[2048,512]{1,0:T(8,128)} async-done(((f32[1024,512]{1,0:T(8,128)}), f32[2048,512]{1,0:T(8,128)}) %all-gather.18.cloned.1.call-update) | async-done | bytes 4194320 | tf_op jit(solution)/shard_map/all_gather | solution.py:25
  302.5 57.7 %all-gather.16.cloned.1.call-done = f32[1024,2048]{1,0:T(8,128)} async-done(((f32[1024,512]{1,0:T(8,128)}), f32[1024,2048]{1,0:T(8,128)}) %all-gather.16.cloned.1.call-update) | async-done | bytes 8388624 | tf_op jit(solution)/shard_map/all_gather | solution.py:24
  360.2 0.0 copy-done.2
  360.2 19.1 %fusion.3 = (f32[]{:T(128)}, f32[]{:T(128)}, f32[]{:T(128)}, f32[1024,512]{1,0:T(8,128)}) fusion(f32[1024,512]{1,0:T(8,128)S(1)} %copy-done.2, s32[512]{0:T(512)S(1)} %iota_add_fusion.1, s32[1024]{0:T(1024)S(1)} %iota_add_fusion, f32[1024,2048]{1,0:T(8,128)} %all-gather.16.cloned.1.call-done, f32[2048,512]{1,0:T(8,128)} %all-gather.18.cloned.1.call-done), kind=kOutput, calls=%fused_computation.8 | convolution fusion | flops 12888571904 | bytes 16783372 | tf_op jit(solution)/shard_map/dot_general | solution.py:26
  379.3 0.0 all-gather.20.cloned.1.call-update
  379.4 0.0 all-gather.24.cloned.1.call-start
  379.4 2.0 pad_maximum_fusion.1
  381.4 22.8 %psum.37 = f32[3]{0:T(128)S(1)} all-reduce(f32[3]{0:T(128)S(1)} %pad_maximum_fusion.1), channel_id=1, replica_groups=mesh['spin'=1,'row'=2,'col'=4] {'row','col'}, use_global_device_ids=true, to_apply=%region_9.10 | all-reduce | flops 3 | bytes 24 | tf_op jit(solution)/shard_map/psum | solution.py:30
  404.2 0.7 fusion.6
  407.5 28.6 %all-gather.20.cloned.1.call-done = f32[1024,2048]{1,0:T(8,128)} async-done(((f32[1024,512]{1,0:T(8,128)}), f32[1024,2048]{1,0:T(8,128)}) %all-gather.20.cloned.1.call-update) | async-done | bytes 8388624 | tf_op jit(solution)/shard_map/all_gather | solution.py:27
  436.1 18.5 %subtract_divide_fusion.1 = f32[1024,512]{1,0:T(8,128)} fusion(f32[1024,512]{1,0:T(8,128)} %get-tuple-element.23, f32[1024,512]{1,0:T(8,128)S(1)} %copy-done.2, f32[1024,2048]{1,0:T(8,128)} %all-gather.20.cloned.1.call-done, f32[2048,512]{1,0:T(8,128)} %all-gather.18.cloned.1.call-done, f32[]{:T(128)} %bitcast.14, f32[]{:T(128)} %bitcast.13, f32[]{:T(128)} %bitcast.12), kind=kOutput, calls=%fused_computation.14 | convolution fusion | flops 12887523328 | bytes 18874380 | tf_op jit(solution)/shard_map/dot_general | solution.py:28
  454.6 0.0 copy-start
  454.6 0.0 all-gather.24.cloned.1.call-update
  454.6 0.0 all-gather.22.cloned.1.call-start
  454.7 0.7 all-gather.22.cloned.1.call-update
  455.4 0.3 all-gather.26.cloned.1.call-start
  455.7 53.5 %all-gather.24.cloned.1.call-done = f32[2048,512]{1,0:T(8,128)} async-done(((f32[1024,512]{1,0:T(8,128)}), f32[2048,512]{1,0:T(8,128)}) %all-gather.24.cloned.1.call-update) | async-done | bytes 4194320 | tf_op jit(solution)/shard_map/all_gather | solution.py:25
  509.1 57.9 %all-gather.22.cloned.1.call-done = f32[1024,2048]{1,0:T(8,128)} async-done(((f32[1024,512]{1,0:T(8,128)}), f32[1024,2048]{1,0:T(8,128)}) %all-gather.22.cloned.1.call-update) | async-done | bytes 8388624 | tf_op jit(solution)/shard_map/all_gather | solution.py:24
  567.0 0.0 copy-done
  567.0 19.1 %fusion.4 = (f32[]{:T(128)}, f32[]{:T(128)}, f32[]{:T(128)}, f32[1024,512]{1,0:T(8,128)}) fusion(f32[1024,512]{1,0:T(8,128)S(1)} %copy-done, s32[512]{0:T(512)S(1)} %iota_add_fusion.1, s32[1024]{0:T(1024)S(1)} %iota_add_fusion, f32[1024,2048]{1,0:T(8,128)} %all-gather.22.cloned.1.call-done, f32[2048,512]{1,0:T(8,128)} %all-gather.24.cloned.1.call-done), kind=kOutput, calls=%fused_computation.9 | convolution fusion | flops 12888571904 | bytes 16783372 | tf_op jit(solution)/shard_map/dot_general | solution.py:26
  586.1 0.0 all-gather.26.cloned.1.call-update
  586.1 2.0 pad_maximum_fusion.2
  588.1 22.8 %psum.38 = f32[3]{0:T(128)S(1)} all-reduce(f32[3]{0:T(128)S(1)} %pad_maximum_fusion.2), channel_id=1, replica_groups=mesh['spin'=1,'row'=2,'col'=4] {'row','col'}, use_global_device_ids=true, to_apply=%region_13.14 | all-reduce | flops 3 | bytes 24 | tf_op jit(solution)/shard_map/psum | solution.py:30
  610.9 0.7 fusion.5
  614.2 28.7 %all-gather.26.cloned.1.call-done = f32[1024,2048]{1,0:T(8,128)} async-done(((f32[1024,512]{1,0:T(8,128)}), f32[1024,2048]{1,0:T(8,128)}) %all-gather.26.cloned.1.call-update) | async-done | bytes 8388624 | tf_op jit(solution)/shard_map/all_gather | solution.py:27
  642.9 19.7 %multiply_reduce_fusion = (f32[]{:T(128)}, f32[1024,512]{1,0:T(8,128)}) fusion(f32[1024,512]{1,0:T(8,128)} %param.3, f32[]{:T(128)} %bitcast.20, f32[1024,2048]{1,0:T(8,128)} %all-gather.26.cloned.1.call-done, f32[2048,512]{1,0:T(8,128)} %all-gather.24.cloned.1.call-done, f32[1024,512]{1,0:T(8,128)} %get-tuple-element.24, f32[]{:T(128)} %bitcast.19, ...), kind=kOutput, calls=%fused_computation.10 | convolution fusion | flops 12888571904 | bytes 20971536 | tf_op jit(solution)/shard_map/dot_general | solution.py:28
  662.6 22.6 %psum.39 = f32[]{:T(128)} all-reduce(f32[]{:T(128)} %get-tuple-element.25), channel_id=1, replica_groups=mesh['spin'=1,'row'=2,'col'=4] {'row','col'}, use_global_device_ids=true, to_apply=%region_15.16 | all-reduce | flops 1 | bytes 8 | tf_op jit(solution)/shard_map/psum | solution.py:33
  (2 shorter events, 0.0 us)
Async XLA Ops:
  7.2 31.6 %copy-start.3 = (f32[1024,512]{1,0:T(8,128)S(1)}, f32[1024,512]{1,0:T(8,128)}, u32[]{:S(2)}) copy-start(f32[1024,512]{1,0:T(8,128)} %param.3) | copy-start | bytes 6291460
  7.2 28.3 %copy-start.4 = (f32[2]{0:T(128)S(1)}, f32[2]{0:T(128)}, u32[]{:S(2)}) copy-start(f32[2]{0:T(128)} %param.4) | copy-start | bytes 28
  7.2 88.6 %all-gather.12.cloned.1.call-start = ((), (), s32[]{:S(2)}) async-start(), calls=%async_computation.1 | async-start | bytes 6291456 | tf_op jit(solution)/shard_map/all_gather | solution.py:25
  40.4 113.2 %copy-start.1 = (f32[1024,512]{1,0:T(8,128)S(1)}, f32[1024,512]{1,0:T(8,128)}, u32[]{:S(2)}) copy-start(f32[1024,512]{1,0:T(8,128)} %fusion.1) | copy-start | bytes 6291460
  40.4 113.2 %all-gather.10.cloned.1.call-start = ((), (), s32[]{:S(2)}) async-start(), calls=%async_computation | async-start | bytes 10485760 | tf_op jit(solution)/shard_map/all_gather | solution.py:24
  41.2 188.3 %all-gather.14.cloned.1.call-start = ((), (), s32[]{:S(2)}) async-start(), calls=%async_computation.2 | async-start | bytes 10485760 | tf_op jit(solution)/shard_map/all_gather | solution.py:27
  172.7 129.8 %all-gather.18.cloned.1.call-start = ((), (), s32[]{:S(2)}) async-start(), calls=%async_computation.4 | async-start | bytes 6291456 | tf_op jit(solution)/shard_map/all_gather | solution.py:25
  248.0 112.2 %copy-start.2 = (f32[1024,512]{1,0:T(8,128)S(1)}, f32[1024,512]{1,0:T(8,128)}, u32[]{:S(2)}) copy-start(f32[1024,512]{1,0:T(8,128)} %subtract_divide_fusion.2) | copy-start | bytes 6291460
  248.0 112.2 %all-gather.16.cloned.1.call-start = ((), (), s32[]{:S(2)}) async-start(), calls=%async_computation.3 | async-start | bytes 10485760 | tf_op jit(solution)/shard_map/all_gather | solution.py:24
  248.6 187.5 %all-gather.20.cloned.1.call-start = ((), (), s32[]{:S(2)}) async-start(), calls=%async_computation.5 | async-start | bytes 10485760 | tf_op jit(solution)/shard_map/all_gather | solution.py:27
  379.4 129.8 %all-gather.24.cloned.1.call-start = ((), (), s32[]{:S(2)}) async-start(), calls=%async_computation.7 | async-start | bytes 6291456 | tf_op jit(solution)/shard_map/all_gather | solution.py:25
  454.6 112.4 %copy-start = (f32[1024,512]{1,0:T(8,128)S(1)}, f32[1024,512]{1,0:T(8,128)}, u32[]{:S(2)}) copy-start(f32[1024,512]{1,0:T(8,128)} %subtract_divide_fusion.1) | copy-start | bytes 6291460
  454.6 112.4 %all-gather.22.cloned.1.call-start = ((), (), s32[]{:S(2)}) async-start(), calls=%async_computation.6 | async-start | bytes 10485760 | tf_op jit(solution)/shard_map/all_gather | solution.py:24
  455.4 187.5 %all-gather.26.cloned.1.call-start = ((), (), s32[]{:S(2)}) async-start(), calls=%async_computation.8 | async-start | bytes 10485760 | tf_op jit(solution)/shard_map/all_gather | solution.py:27
Sparse Core Ops, SparseCore 0:
  40.6 55.1 all-gather.11
  97.9 55.7 all-gather.9
  172.9 56.5 all-gather.13
  248.1 54.3 all-gather.17
  304.5 55.7 all-gather.15
  379.5 56.5 all-gather.19
  454.8 54.3 all-gather.23
  511.2 55.7 all-gather.21
  586.2 56.5 all-gather.25
where the time goes:
time: 695 us; the launch traced here: 693 us
  waiting for transfers between devices  423 us (61%)
  blocking collectives  116 us (17%)
  matrix products  114 us (16%)
  between operations  26.3 us (4%)
  other arithmetic  10.6 us (2%)
    all_gather x3, waiting for transfers between devices, local_fn(): x_rows = lax.all_gather(density, 'col', axis=1, tiled=True)  173 us
    all_gather x3, waiting for transfers between devices, local_fn(): x_cols = lax.all_gather(density, 'row', axis=0, tiled=True)  162 us
    all_gather x3, waiting for transfers between devices, local_fn(): sq_rows = lax.all_gather(dens_sq, 'col', axis=1, tiled=True)  85.9 us
    psum x3, blocking collectives, local_fn(): traces = lax.psum(part_sums, ('row', 'col'))  68.3 us
    dot_general x3, matrix products, local_fn(): jnp.dot(x_rows, x_cols, precision=highest, preferred_element_type=jnp.flo...  57.3 us
    dot_general x3, matrix products, local_fn(): jnp.dot(sq_rows, x_cols, precision=highest, preferred_element_type=jnp.fl...  56.7 us
    psum x1, blocking collectives, local_fn(): lax.psum(jnp.sum(jnp.where(diag_mask, ham_blk, 0.0)), ('row', 'col'))  25.3 us
    psum x1, blocking collectives, local_fn(): energy = 2.0 * lax.psum(jnp.sum(density * ham_blk), ('row', 'col'))  22.6 us
  transfers between devices with their start and end apart: 9, of which 9 were waited for; matrix products, arithmetic and copies ran while one was open for 1% of the time, Pallas kernels for 0%

commit v1 on v0

v1 whole, which is shorter than its diff:
```python
import jax
import jax.numpy as jnp
from jax import lax
from jax.experimental import pallas as pl
from jax.experimental.pallas import tpu as pltpu
from jax.sharding import PartitionSpec as P

STEPS = 3
PANELS = 8
SLOTS = 5
MESH = pl.DeviceIdType.MESH
NN = (((1,), (0,)), ((), ()))
NT = (((1,), (1,)), ((), ()))


def dot(lhs, rhs, dims):
    return lax.dot_general(lhs, rhs, dims, precision=lax.Precision.HIGHEST, preferred_element_type=jnp.float32)


def pick(index, values):
    return sum(jnp.where(index == k, v, 0) for k, v in enumerate(values))


def flip(bit, by):
    return bit + by - 2 * bit * by


def same(a, b):
    return 1 - (a - b) * (a - b)


def panel_of(x, y, c):
    return 4 * x + 2 * c + y


def h_block(x, y, c, t):
    col_off = t // 2
    row_off = 2 * (t % 2) + flip(col_off, y)
    tables = (
        (0, 0, (1, 1, 3, 0, 2), (1, 0, 0, 0, 0)),
        (0, 1, (3, 3, 1, 1, 2), (1, 0, 0, 1, 0)),
        (1, 0, (0, 1, 2, 3, 1), (0, 0, 0, 0, 1)),
        (1, 1, (2, 3, 1, 3, 1), (0, 0, 0, 1, 1)),
    )
    row_on = sum(same(x, tx) * same(c, tc) * pick(t, rows) for tx, tc, rows, _ in tables)
    col_on = sum(same(x, tx) * same(c, tc) * pick(t, cols) for tx, tc, _, cols in tables)
    on = same(x, y)
    return on * row_on + (1 - on) * row_off, on * col_on + (1 - on) * col_off


def kernel(n, bounds, n_occ, h_ref, out_ref, e_ref, buf, hrow, xrow, x2row, acc, parts, coef, sums, send_sem, recv_sem, part_send, part_recv):
    blk_n = n // PANELS
    y = lax.axis_index("row")
    j = lax.axis_index("col")
    x, c = j // 2, j % 2
    me = panel_of(x, y, c)

    def bits(mask):
        return flip(x, mask // 4), flip(y, mask % 2), flip(c, (mask // 2) % 2)

    def device(mask):
        dx, dy, dc = bits(mask)
        return (0, dy, 2 * dx + dc)

    def panel(mask):
        return panel_of(*bits(mask))

    PARTNER, XN, YN, DIAG = 2, 4, 1, 5

    barrier = pltpu.get_barrier_semaphore()
    for mask in range(1, 8):
        pl.semaphore_signal(barrier, inc=1, device_id=device(mask), device_id_type=MESH)
    pl.semaphore_wait(barrier, 7)

    def send(src, buf_id, q, t, way):
        mask = (PARTNER, XN, YN)[way]
        return pltpu.make_async_remote_copy(
            src_ref=src,
            dst_ref=buf.at[buf_id, q, t],
            send_sem=send_sem.at[buf_id, q, t, way],
            recv_sem=recv_sem.at[buf_id, q, t],
            device_id=device(mask),
            device_id_type=MESH,
        )

    def x_first(t, src_y):
        return jnp.where(t == 4, 1 - src_y, 1 - t % 2)

    def forward(buf_id, mask, t, act):
        q = panel(mask)
        block = buf.at[buf_id, q, t]
        if mask in (XN, YN, DIAG):
            act(send(block, buf_id, q, t, 0))
        if mask == XN:

            @pl.when(x_first(t, y) == 1)
            def _():
                act(send(block, buf_id, q, t, 2))

        if mask == YN:

            @pl.when(x_first(t, 1 - y) == 0)
            def _():
                act(send(block, buf_id, q, t, 1))

    def arrive(buf_id, mask, t):
        if mask != 0:
            q = panel(mask)
            send(buf.at[buf_id, q, t], buf_id, q, t, 0).wait_recv()
            forward(buf_id, mask, t, lambda copy: copy.start())

    def drain(buf_id, valid, own_src):
        @pl.loop(0, SLOTS)
        def _(t):
            @pl.when(valid(0, t))
            def _():
                for way in range(3):
                    send(own_src(t), buf_id, me, t, way).wait_send()

            for mask in (XN, YN, DIAG):

                @pl.when(valid(mask, t))
                def _():
                    forward(buf_id, mask, t, lambda copy: copy.wait_send())

    def valid_h(mask, t):
        qx, qy, _ = bits(mask)
        return jnp.logical_or(t < 4, same(qx, qy) == 1)

    def valid_x(mask, t):
        qx, _, qc = bits(mask)
        return jnp.logical_or(t < 4, same(qx, qc) == 1)

    def part_copy(rnd, src, mask):
        return pltpu.make_async_remote_copy(
            src_ref=parts.at[rnd, src],
            dst_ref=parts.at[rnd, src],
            send_sem=part_send.at[rnd, mask],
            recv_sem=part_recv.at[rnd, src],
            device_id=device(mask),
            device_id_type=MESH,
        )

    def sum_start(rnd, vals):
        for k, val in enumerate(vals):
            parts[rnd, me, k] = val
        for mask in range(1, 8):
            part_copy(rnd, me, mask).start()

    def sum_finish(rnd, count):
        for mask in range(1, 8):
            part_copy(rnd, panel(mask), mask).wait_recv()
        for mask in range(1, 8):
            part_copy(rnd, me, mask).wait_send()
        out = []
        for k in range(count):
            tot = parts[rnd, 0, k]
            for q in range(1, PANELS):
                tot = tot + parts[rnd, q, k]
            out.append(jnp.sum(jnp.sum(tot, axis=1, keepdims=True), axis=0, keepdims=True))
        return out

    def fold(val):
        rows, cols = val.shape
        val = jnp.sum(val.reshape(rows // 8, 8, cols), axis=0)
        tot = val[:, :128]
        for k in range(1, cols // 128):
            tot = tot + val[:, k * 128 : (k + 1) * 128]
        return tot

    def h_src(t):
        a, b = h_block(x, y, c, t)
        return h_ref.at[pl.ds(pl.multiple_of(a * blk_n, blk_n), blk_n), pl.ds(pl.multiple_of(b * blk_n, blk_n), blk_n)]

    HB, LAST = 2, 0

    @pl.loop(0, SLOTS)
    def _(t):
        @pl.when(valid_h(0, t))
        def _():
            for way in range(3):
                send(h_src(t), HB, me, t, way).start()

    rows_n, cols_n = h_ref.shape
    mu_part = jnp.zeros((8, 128), jnp.float32)
    for k in range(rows_n // blk_n):
        tile = h_ref[k * blk_n : (k + 1) * blk_n, :]
        row_ids = y * rows_n + k * blk_n + lax.broadcasted_iota(jnp.int32, tile.shape, 0)
        col_ids = j * cols_n + lax.broadcasted_iota(jnp.int32, tile.shape, 1)
        mu_part = mu_part + fold(jnp.where(row_ids == col_ids, tile, 0.0))
    sum_start(0, [mu_part])

    eye = (lax.broadcasted_iota(jnp.int32, (blk_n, blk_n), 0) == lax.broadcasted_iota(jnp.int32, (blk_n, blk_n), 1)).astype(jnp.float32)
    (trace_h,) = sum_finish(0, 1)
    occ = n_occ[0].astype(jnp.float32)
    mu = trace_h / n
    lam = jnp.minimum(occ / (bounds[1] - mu), (n - occ) / (mu - bounds[0]))
    coef[0:1, :] = jnp.broadcast_to(lam / n, (1, blk_n))
    coef[1:2, :] = jnp.broadcast_to(mu, (1, blk_n))
    coef[2:3, :] = jnp.broadcast_to(jnp.full((1, 1), occ / n, jnp.float32), (1, blk_n))

    def first_x(mask, t):
        qx, qy, qc = bits(mask)
        a, b = h_block(qx, qy, qc, t)
        row, col = 4 * qy + a, 4 * qx + 2 * qc + b
        blk = h_src(t)[...] if mask == 0 else buf[HB, panel(mask), t]
        diag = eye * (row == col).astype(jnp.float32)
        val = coef[0:1, :] * (coef[1:2, :] * diag - blk) + coef[2:3, :] * diag
        diff = (col - row + 8) % 8

        @pl.when(diff <= 4)
        def _():
            buf[0, row, diff] = val

        @pl.when(diff >= 4)
        def _():
            buf[0, col, (8 - diff)] = val.T

        @pl.when(row == me)
        def _():
            hrow[col] = blk
            xrow[col] = val

        @pl.when(jnp.logical_and(col == me, row != me))
        def _():
            hrow[row] = blk.T
            xrow[row] = val.T

    def own_h(src_mask, t):
        return None

    @pl.loop(0, SLOTS)
    def _(t):
        for mask in (0, 2, 4, 1, 6, 3):

            @pl.when(valid_h(mask, t))
            def _():
                arrive(HB, mask, t)
                first_x(mask, t)

    @pl.loop(0, SLOTS)
    def _(t):
        for mask in (5, 7):

            @pl.when(valid_h(mask, t))
            def _():
                arrive(HB, mask, t)
                first_x(mask, t)

    def product(left, b, col):
        tot = dot(left[col], buf[b, col, 0], NN)
        for d in range(1, 4):
            k = (col + 8 - d) % 8
            tot = tot + dot(left[k], buf[b, k, d], NN)
        k = (col + 4) % 8
        tot = tot + dot(left[k], buf[b, k, 4], NN)
        for d in range(1, 4):
            k = (col + d) % 8
            tot = tot + dot(left[k], buf[b, col, d], NT)
        return tot

    @pl.loop(0, PANELS)
    def _(col):
        x2row[col] = product(xrow, 0, col)

    def traces(rnd):
        t1 = fold(xrow[me] * eye)
        sums[...] = jnp.zeros_like(sums)

        @pl.loop(0, PANELS)
        def _(col):
            xv = xrow[col]
            sums[0] += fold(xv * xv)
            sums[1] += fold(xv * x2row[col])

        sum_start(rnd, [t1, sums[0], sums[1]])

    def mix(rnd):
        t1, t2, t3 = sum_finish(rnd, 3)
        cval = (t2 - t3) / (t1 - t2)
        for k, val in enumerate((1.0 - 2.0 * cval, 1.0 + cval, 1.0 - cval)):
            coef[k : k + 1, :] = jnp.broadcast_to(val, (1, blk_n))

    def updated(col):
        return (coef[0:1, :] * xrow[col] + coef[1:2, :] * x2row[col] - acc[...]) / coef[2:3, :]

    for step in range(STEPS - 1):
        old, new = step, step + 1
        traces(1 + step)

        @pl.loop(0, PANELS)
        def _(d):
            col = (me + d) % 8
            acc[...] = product(x2row, old, col)

            @pl.when(d == 0)
            def _():
                if step == 0:
                    drain(HB, valid_h, h_src)
                else:
                    drain(old, valid_x, lambda t: buf.at[old, me, t])
                mix(1 + step)

            val = updated(col)

            @pl.when(d <= 4)
            def _():
                buf[new, me, d] = val

            xrow[col] = val

            @pl.when(jnp.logical_and(d <= 4, valid_x(0, d)))
            def _():
                for way in range(3):
                    send(buf.at[new, me, d], new, me, d, way).start()

        @pl.loop(0, PANELS)
        def _(col):
            x2row[col] = jnp.zeros((blk_n, blk_n), jnp.float32)

        def use(mask, t):
            q = panel(mask)
            col = (q + t) % 8
            blk = buf[new, q, t]
            x2row[col] += dot(xrow[q], blk, NN)

            @pl.when(t > 0)
            def _():
                x2row[q] += dot(xrow[col], blk, NT)

            @pl.when(t == 4)
            def _():
                buf[new, col, 4] = blk.T

        for masks in ((0, 2, 4, 1, 6, 3), (5, 7)):

            @pl.loop(0, SLOTS)
            def _(t):
                for mask in masks:

                    @pl.when(valid_x(mask, t))
                    def _():
                        arrive(new, mask, t)
                        use(mask, t)

    old = STEPS - 1
    traces(STEPS)
    sums[2] = jnp.zeros((8, 128), jnp.float32)

    def last_copy(i):
        return pltpu.make_async_remote_copy(
            src_ref=buf.at[LAST, me, i],
            dst_ref=buf.at[LAST, me, i],
            send_sem=send_sem.at[LAST, me, i, 0],
            recv_sem=recv_sem.at[LAST, me, i],
            device_id=device(YN),
            device_id_type=MESH,
        )

    def place(i, b, val):
        out_ref[pl.ds(pl.multiple_of(i * blk_n, blk_n), blk_n), pl.ds(pl.multiple_of(b * blk_n, blk_n), blk_n)] = val.T

    @pl.loop(0, PANELS)
    def _(d):
        half, i = d // 4, d % 4
        col = 4 * flip(y, 1 - half) + i
        acc[...] = product(x2row, old, col)

        @pl.when(d == 0)
        def _():
            drain(old, valid_x, lambda t: buf.at[old, me, t])
            mix(STEPS)

        val = updated(col)

        @pl.when(half == 0)
        def _():
            buf[LAST, me, i] = val

        sums[2] += fold(val * hrow[col])

        @pl.when(half == 0)
        def _():
            last_copy(i).start()

        @pl.when(half == 1)
        def _():
            place(i, y, val)

    sum_start(STEPS + 1, [sums[2]])

    @pl.loop(0, 4)
    def _(i):
        q = panel(YN)
        pltpu.make_async_remote_copy(
            src_ref=buf.at[LAST, q, i],
            dst_ref=buf.at[LAST, q, i],
            send_sem=send_sem.at[LAST, q, i, 0],
            recv_sem=recv_sem.at[LAST, q, i],
            device_id=device(YN),
            device_id_type=MESH,
        ).wait_recv()
        place(i, 1 - y, buf[LAST, q, i])

    @pl.loop(0, 4)
    def _(i):
        last_copy(i).wait_send()

    (energy,) = sum_finish(STEPS + 1, 1)
    e_ref[0] = 2.0 * jnp.sum(energy)


def solution(mesh):
    n_cols = mesh.shape["col"]

    def local_fn(ham_blk, bounds, n_occ):
        rows_n, cols_n = ham_blk.shape
        n = cols_n * n_cols
        blk_n = n // PANELS
        f32 = jnp.float32
        return pl.pallas_call(
            lambda *refs: kernel(n, *refs),
            out_shape=(jax.ShapeDtypeStruct((rows_n, cols_n), f32), jax.ShapeDtypeStruct((1,), f32)),
            in_specs=[
                pl.BlockSpec(memory_space=pltpu.SMEM),
                pl.BlockSpec(memory_space=pltpu.SMEM),
                pl.BlockSpec(memory_space=pltpu.VMEM),
            ],
            out_specs=(pl.BlockSpec(memory_space=pltpu.VMEM), pl.BlockSpec(memory_space=pltpu.SMEM)),
            scratch_shapes=[
                pltpu.VMEM((3, PANELS, SLOTS, blk_n, blk_n), f32),
                pltpu.VMEM((PANELS, blk_n, blk_n), f32),
                pltpu.VMEM((PANELS, blk_n, blk_n), f32),
                pltpu.VMEM((PANELS, blk_n, blk_n), f32),
                pltpu.VMEM((blk_n, blk_n), f32),
                pltpu.VMEM((STEPS + 2, PANELS, 3, 8, 128), f32),
                pltpu.VMEM((8, blk_n), f32),
                pltpu.VMEM((3, 8, 128), f32),
                pltpu.SemaphoreType.DMA((3, PANELS, SLOTS, 3)),
                pltpu.SemaphoreType.DMA((3, PANELS, SLOTS)),
                pltpu.SemaphoreType.DMA((STEPS + 2, PANELS)),
                pltpu.SemaphoreType.DMA((STEPS + 2, PANELS)),
            ],
            compiler_params=pltpu.CompilerParams(collective_id=0, has_side_effects=True, vmem_limit_bytes=60 << 20),
            name="purify",
        )(bounds, n_occ, ham_blk)

    spec_mat = P(("spin", "row"), "col")
    return jax.shard_map(local_fn, mesh=mesh, in_specs=(spec_mat, P("spin"), P("spin")), out_specs=(spec_mat, P("spin")), check_vma=False)
```

time: 695 us -> 219 us (0.32)
  waiting for transfers between devices: 423 us -> 0 us
  Pallas kernels: 0 us -> 212 us
  blocking collectives: 116 us -> 0 us
  matrix products: 114 us -> 0 us
  between operations: 26.3 us -> 3.02 us
  other arithmetic: 10.6 us -> 0 us
    all_gather x9 -> x0, waiting for transfers between devices: 421 us -> none  [the longest x3 173 us: local_fn(): x_rows = lax.all_gather(density, 'col', axis=1, tiled=True)]
    pallas_call x0 -> x1, Pallas kernels: none -> 212 us  [local_fn(): pl.pallas_call(lambda *refs: kernel(n, *refs), out_shape=(jax.ShapeDtypeS...]
    psum x5 -> x0, blocking collectives: 116 us -> none  [the longest x3 68.3 us: local_fn(): traces = lax.psum(part_sums, ('row', 'col'))]
    dot_general x6 -> x0, matrix products: 114 us -> none  [the longest x3 57.3 us: local_fn(): jnp.dot(x_rows, x_cols, precision=highest, preferred_element_type=jnp.flo...]
  transfers between devices with their start and end apart: 9 -> 0, of which waited for: 9 -> 0; matrix products, arithmetic and copies ran while one was open for 1% -> 0% of each run, Pallas kernels for 0% -> 0%
where the time goes in v1:
time: 219 us; the launch traced here: 218 us
  Pallas kernels  212 us (97%)
  local copies, waits for them, and re-layouts  3.08 us (1%)
  between operations  3.02 us (1%)
    pallas_call x1, Pallas kernels, local_fn(): pl.pallas_call(lambda *refs: kernel(n, *refs), out_shape=(jax.ShapeDtypeS...  212 us

profile of v1, /device:TPU:0, one launch (start us, length us, event | category | flops | bytes accessed | tf_op | source)
XLA Modules:
  0.0 218.4 jit_solution(17486895544089812067)
XLA Ops:
  1.3 212.3 %purify.1 = (f32[1024,512]{1,0:T(8,128)}, f32[1]{0:T(128)}) custom-call(f32[2]{0:T(128)} %refs_0_.1, s32[1]{0:T(128)S(6)} %copy.7.refs_1_, f32[1024,512]{1,0:T(8,128)} %refs_2_.1), custom_call_target="tpu_custom_call" | custom-call | tf_op jit(solution)/shard_map/purify/pallas_call | solution.py:421
  213.6 3.1 %copy.8 = f32[1024,512]{1,0:T(8,128)} copy(f32[1024,512]{1,0:T(8,128)} %get-tuple-element.4) | data formatting | bytes 4194304

commit v2 on v0

v2 whole, which is shorter than its diff:
```python
import jax
import jax.numpy as jnp
from jax import lax
from jax.experimental import pallas as pl
from jax.experimental.pallas import tpu as pltpu
from jax.sharding import PartitionSpec as P

STEPS = 3
PANELS = 8
SLOTS = 5
MESH = pl.DeviceIdType.MESH
NN = (((1,), (0,)), ((), ()))
NT = (((1,), (1,)), ((), ()))


def dot(lhs, rhs, dims):
    return lax.dot_general(lhs, rhs, dims, precision=lax.Precision.HIGHEST, preferred_element_type=jnp.float32)


def flag(cond):
    return lax.convert_element_type(cond, jnp.int32)


def pick(index, values):
    return sum(flag(index == k) * v for k, v in enumerate(values) if v)


def half(val, by=2):
    return lax.div(val, jnp.int32(by))


def part(val, by=2):
    return lax.rem(val, jnp.int32(by))


def flip(bit, by):
    return bit + by - 2 * bit * by


def panel_bits(q):
    return q // 4, q % 2, (q // 2) % 2


def packed(digits, base):
    return sum(d * base**k for k, d in enumerate(digits))


def h_blocks(q):
    x, y, c = panel_bits(q)
    if x == y:
        local = {
            (0, 0): ((1, 1), (1, 0), (3, 0), (0, 0), (2, 0)),
            (0, 1): ((3, 1), (3, 0), (1, 0), (1, 1), (2, 0)),
            (1, 0): ((0, 0), (1, 0), (2, 0), (3, 0), (1, 1)),
            (1, 1): ((2, 0), (3, 0), (1, 0), (3, 1), (1, 1)),
        }[x, c]
    else:
        local = tuple((2 * k + (b + y) % 2, b) for b in range(2) for k in range(2))
    return tuple((4 * y + a, 4 * x + 2 * c + b) for a, b in local)


def x_blocks(q):
    x, y, c = panel_bits(q)
    return tuple(q ^ m for m in (4 + 2 * x, 1 + 2 * y, 5 + 2 * y, 0, 2, 7 - 2 * y))


def kernel(n, bounds, n_occ, h_ref, out_ref, e_ref, buf, hrow, x2row, acc, parts, coef, sums, send_sem, recv_sem, part_send, part_recv, last_send, last_recv):
    blk_n = n // PANELS
    y = lax.axis_index("row")
    j = lax.axis_index("col")
    x, c = half(j), part(j)
    me = 4 * x + 2 * c + y
    on = 1 - flip(x, y)

    class Source:
        def __init__(self, q, h_pack, h_count, x_pack, x_count):
            self.fields = q, h_pack, h_count, x_pack, x_count
            self.q, self.h_pack, self.h_count, self.x_pack, self.x_count = self.fields

        def __add__(self, other):
            return Source(*(a + b for a, b in zip(self.fields, other.fields)))

        def __mul__(self, by):
            return Source(*(a * by for a in self.fields))

    def device(mask):
        dx, dy, dc = flip(x, half(mask, 4)), flip(y, part(mask)), flip(c, part(half(mask)))
        return (0, dy, 2 * dx + dc)

    def source(mask):
        q = panel(mask)
        return Source(
            q,
            pick(q, [packed([8 * row + col for row, col in h_blocks(k)], 64) for k in range(PANELS)]),
            pick(q, [len(h_blocks(k)) for k in range(PANELS)]),
            pick(q, [packed(x_blocks(k), 8) for k in range(PANELS)]),
            pick(q, [5 - (k // 2) % 2 for k in range(PANELS)]),
        )

    def panel(mask):
        return 4 * flip(x, mask // 4) + 2 * flip(c, (mask // 2) % 2) + flip(y, mask % 2)

    def h_place(src, t):
        code = part(lax.div(src.h_pack, pick(t, [64**k for k in range(SLOTS)])), 64)
        return half(code, 8), part(code, 8)

    def x_place(src, t):
        return src.q, part(lax.div(src.x_pack, pick(t, [8**k for k in range(SLOTS + 1)])), 8)

    devices = [device(jnp.int32(mask)) for mask in range(8)]
    sources = [source(mask) for mask in range(8)]

    PARTNER, XN, YN, DIAG = 2, 4, 1, 5

    barrier = pltpu.get_barrier_semaphore()
    for mask in range(1, 8):
        pl.semaphore_signal(barrier, inc=1, device_id=devices[mask], device_id_type=MESH)
    pl.semaphore_wait(barrier, 7)

    class Exchange:
        def __init__(self, rnd, buf_id, place, count, own_src=None):
            self.rnd, self.buf_id, self.place, self.count = rnd, buf_id, place, count
            self.own_src = own_src or (lambda row, col: buf.at[buf_id, row, col])

        def copy(self, at, t, way, src=None):
            q, row, col = at
            block = buf.at[self.buf_id, row, col]
            return pltpu.make_async_remote_copy(
                src_ref=block if src is None else src,
                dst_ref=block,
                send_sem=send_sem.at[self.rnd, q, t, way],
                recv_sem=recv_sem.at[self.rnd, q, t],
                device_id=devices[(PARTNER, XN, YN)[way]],
                device_id_type=MESH,
            )

        def own(self, at, t, act):
            for way in range(3):
                act(self.copy(at, t, way, self.own_src(*at[1:])))

        def forward(self, mask, at, t, act):
            if mask in (XN, YN, DIAG):
                act(self.copy(at, t, 0))
            if mask == XN:

                @pl.when(part(t) + flag(t == 4) * y == 0)
                def _():
                    act(self.copy(at, t, 2))

            if mask == YN:

                @pl.when(part(t) + flag(t == 4) * (1 - y) == 1)
                def _():
                    act(self.copy(at, t, 1))

        def arrive(self, mask, at, t):
            self.copy(at, t, 0).wait_recv()
            self.forward(mask, at, t, lambda copy: copy.start())

        def at(self, src, t):
            return (src.q, *self.place(src, t))

        def each(self, jobs, first=0, last=SLOTS):
            @pl.loop(0, last - first)
            def _(i):
                t = i + first
                for mask, body in jobs:
                    src = mask if isinstance(mask, Source) else sources[mask]

                    @pl.when(t < self.count(src))
                    def _():
                        body(mask, self.at(src, t), t)

        def drain(self):
            def fwd(mask, at, t):
                self.forward(mask, at, t, lambda copy: copy.wait_send())

            self.each([(0, lambda mask, at, t: self.own(at, t, lambda copy: copy.wait_send()))] + [(mask, fwd) for mask in (XN, YN, DIAG)])

    def part_copy(rnd, src, mask):
        return pltpu.make_async_remote_copy(
            src_ref=parts.at[rnd, src],
            dst_ref=parts.at[rnd, src],
            send_sem=part_send.at[rnd, mask],
            recv_sem=part_recv.at[rnd, src],
            device_id=devices[mask],
            device_id_type=MESH,
        )

    def sum_start(rnd, vals):
        for k, val in enumerate(vals):
            parts[rnd, me, k] = val
        for mask in range(1, 8):
            part_copy(rnd, me, mask).start()

    def sum_finish(rnd, count):
        for mask in range(1, 8):
            part_copy(rnd, sources[mask].q, mask).wait_recv()
        for mask in range(1, 8):
            part_copy(rnd, me, mask).wait_send()
        out = []
        for k in range(count):
            tot = parts[rnd, 0, k]
            for q in range(1, PANELS):
                tot = tot + parts[rnd, q, k]
            out.append(jnp.sum(jnp.sum(tot, axis=1, keepdims=True), axis=0, keepdims=True))
        return out

    def fold(val):
        rows, cols = val.shape
        val = jnp.sum(val.reshape(rows // 8, 8, cols), axis=0)
        tot = val[:, :128]
        for k in range(1, cols // 128):
            tot = tot + val[:, k * 128 : (k + 1) * 128]
        return tot

    def span(k):
        return pl.ds(pl.multiple_of(k * blk_n, blk_n), blk_n)

    def clear():
        @pl.loop(0, PANELS)
        def _(col):
            x2row[col] = jnp.zeros((blk_n, blk_n), jnp.float32)

    def h_src(row, col):
        return h_ref.at[span(row - 4 * y), span(col - 2 * j)]

    hx = Exchange(0, 1, h_place, lambda src: src.h_count, h_src)
    hx.each([(0, lambda mask, at, t: hx.own(at, t, lambda copy: copy.start()))])

    rows_n, cols_n = h_ref.shape
    mu_part = jnp.zeros((8, 128), jnp.float32)
    for k in range(rows_n // blk_n):
        tile = h_ref[k * blk_n : (k + 1) * blk_n, :]
        row_ids = y * rows_n + k * blk_n + lax.broadcasted_iota(jnp.int32, tile.shape, 0)
        col_ids = j * cols_n + lax.broadcasted_iota(jnp.int32, tile.shape, 1)
        mu_part = mu_part + fold(jnp.where(row_ids == col_ids, tile, 0.0))
    sum_start(0, [mu_part])
    clear()

    eye = (lax.broadcasted_iota(jnp.int32, (blk_n, blk_n), 0) == lax.broadcasted_iota(jnp.int32, (blk_n, blk_n), 1)).astype(jnp.float32)
    (trace_h,) = sum_finish(0, 1)
    occ = n_occ[0].astype(jnp.float32)
    mu = trace_h / n
    lam = jnp.minimum(occ / (bounds[1] - mu), (n - occ) / (mu - bounds[0]))
    coef[0:1, :] = jnp.broadcast_to(lam / n, (1, blk_n))
    coef[1:2, :] = jnp.broadcast_to(mu, (1, blk_n))
    coef[2:3, :] = jnp.broadcast_to(jnp.full((1, 1), occ / n, jnp.float32), (1, blk_n))

    def first_x(mask, at):
        _, row, col = at
        blk = h_src(row, col)[...] if mask == 0 else buf[1, row, col]
        diag = eye * (row == col).astype(jnp.float32)
        val = coef[0:1, :] * (coef[1:2, :] * diag - blk) + coef[2:3, :] * diag
        buf[0, row, col] = val

        @pl.when(row != col)
        def _():
            buf[0, col, row] = val.T

        @pl.when(row == me)
        def _():
            hrow[col] = blk

        @pl.when(jnp.logical_and(col == me, row != me))
        def _():
            hrow[row] = blk.T

    def use(buf_id, row, col, turn):
        blk = buf[buf_id, row, col]
        x2row[col] += dot(buf[buf_id, me, row], blk, NN)

        @pl.when(row != col)
        def _():
            if turn:
                buf[buf_id, col, row] = blk.T
            x2row[row] += dot(buf[buf_id, me, col], blk, NT)

    def h_take(mask, at, t):
        if mask != 0:
            hx.arrive(mask, at, t)
        first_x(mask, at)

    def h_use(mask, at, t):
        use(0, *at[1:], False)

    def h_both(mask, at, t):
        h_take(mask, at, t)
        h_use(mask, at, t)

    early = [sources[k] * on + sources[XN + k] * (1 - on) for k in (0, PARTNER)]
    late = [sources[k] * (1 - on) + sources[XN + k] * on for k in (0, PARTNER)]
    @pl.loop(0, 4)
    def _(k):
        first_x(0, (me, 4 * y + k, me))

    hx.each([(mask, h_take) for mask in (0, PARTNER)])
    hx.each([(mask, h_take) for mask in (XN, YN, XN + 2, YN + 2)] + [(src, h_use) for src in early])
    hx.each([(src, h_use) for src in late + [sources[YN], sources[YN + 2]]] + [(DIAG, h_take)])
    hx.each([(DIAG, h_use), (DIAG + 2, h_both)])

    def product(old, col):
        tot = dot(x2row[0], buf[old, 0, col], NN)
        for k in range(1, PANELS):
            tot = tot + dot(x2row[k], buf[old, k, col], NN)
        return tot

    def traces(old, rnd):
        t1 = fold(buf[old, me, me] * eye)
        sums[...] = jnp.zeros_like(sums)

        @pl.loop(0, PANELS)
        def _(col):
            xv = buf[old, me, col]
            sums[0] += fold(xv * xv)
            sums[1] += fold(xv * x2row[col])

        sum_start(rnd, [t1, sums[0], sums[1]])

    def mix(rnd):
        t1, t2, t3 = sum_finish(rnd, 3)
        cval = (t2 - t3) / (t1 - t2)
        inv = 1.0 / (1.0 - cval)
        for k, val in enumerate(((1.0 - 2.0 * cval) * inv, (1.0 + cval) * inv, inv)):
            coef[k : k + 1, :] = jnp.broadcast_to(val, (1, blk_n))

    def updated(old, col):
        return coef[0:1, :] * buf[old, me, col] + coef[1:2, :] * x2row[col] - coef[2:3, :] * acc[...]

    before = hx
    for step in range(STEPS - 1):
        old, new = step % 2, (step + 1) % 2
        before.drain()
        traces(old, 1 + step)
        ex = Exchange(1 + step, new, x_place, lambda src: src.x_count)

        @pl.loop(0, SLOTS + 1)
        def _(t):
            at = ex.at(sources[0], t)
            col = at[2]
            acc[...] = product(old, col)

            @pl.when(t == 0)
            def _():
                mix(1 + step)

            buf[new, me, col] = updated(old, col)

            @pl.when(t < sources[0].x_count)
            def _():
                ex.own(at, t, lambda copy: copy.start())

        clear()

        def x_use(mask, at, t):
            use(new, *at[1:], True)

        def x_take(mask, at, t):
            ex.arrive(mask, at, t)
            _, row, col = at

            @pl.when(col == me)
            def _():
                buf[new, me, row] = buf[new, row, col].T

        def x_both(mask, at, t):
            ex.arrive(mask, at, t)
            x_use(mask, at, t)

        near = (PARTNER, XN, YN, XN + 2, YN + 2)
        ex.each([(0, x_use)])
        ex.each([(mask, x_take) for mask in near], 0, 2)
        ex.each([(mask, x_use) for mask in near], 0, 2)
        ex.each([(mask, x_both) for mask in near], 2, SLOTS)
        ex.each([(mask, x_both) for mask in (DIAG, DIAG + 2)])
        before = ex

    old, end = (STEPS - 1) % 2, STEPS % 2
    before.drain()
    traces(old, STEPS)
    sums[2] = jnp.zeros((8, 128), jnp.float32)

    def other(q, mask):
        return 4 * flip(half(q, 4), half(mask, 4)) + 2 * flip(part(half(q)), part(half(mask))) + flip(part(q), part(mask))

    def last_copy(q, mask, to):
        block = buf.at[end, q, other(q, mask)]
        return pltpu.make_async_remote_copy(
            src_ref=block,
            dst_ref=block,
            send_sem=last_send.at[mask],
            recv_sem=last_recv.at[mask],
            device_id=device(to),
            device_id_type=MESH,
        )

    def put(row, b, val):
        out_ref[span(row - 4 * y), span(b)] = val

    def last_mask(d):
        return on * pick(d, (5, 4, 7, 6, 3, 0, 1, 2)) + (1 - on) * pick(d, (0, 2, 4, 5, 6, 7, 1, 3))

    def last_send_to(d):
        return on * pick(d, (4, 1, 6, 1, 2)) + (1 - on)

    def last_sends(d):
        return d < 2 + 3 * on

    @pl.loop(0, PANELS)
    def _(d):
        @pl.when(d < 6 + 2 * on)
        def _():
            mask = last_mask(d)
            col = other(me, mask)
            acc[...] = product(old, col)

            @pl.when(d == 0)
            def _():
                mix(STEPS)

            val = updated(old, col)

            @pl.when(last_sends(d))
            def _():
                buf[end, me, col] = val

            weight = 1 + on * part(mask) * (1 - half(mask, 4))
            sums[2] += fold(val * hrow[col]) * weight.astype(jnp.float32)

            @pl.when(last_sends(d))
            def _():
                last_copy(me, mask, last_send_to(d)).start()

            @pl.when(half(col, 4) == y)
            def _():
                put(col, y, val.T)

            @pl.when(jnp.logical_and(on == 1, mask == 1))
            def _():
                put(me, 1 - y, val)

    sum_start(STEPS + 1, [sums[2]])

    @pl.when(on == 1)
    def _():
        for mask, src in ((3, 2), (0, 1), (2, 1)):
            q = sources[src].q
            last_copy(q, jnp.int32(mask), jnp.int32(src)).wait_recv()
            col = other(q, jnp.int32(mask))
            if mask == 3:
                put(q, 1 - y, buf[end, q, col])
            else:
                put(col, 1 - y, buf[end, q, col].T)

    @pl.when(on == 0)
    def _():
        for mask, src in ((5, 4), (4, 1), (7, 6), (6, 1)):
            q = sources[src].q
            last_copy(q, jnp.int32(mask), jnp.int32(src)).wait_recv()
            col = other(q, jnp.int32(mask))
            if src == YN:
                put(col, 1 - y, buf[end, q, col].T)
            else:
                put(q, 1 - y, buf[end, q, col])

    @pl.loop(0, SLOTS)
    def _(d):
        @pl.when(last_sends(d))
        def _():
            last_copy(me, last_mask(d), last_send_to(d)).wait_send()

    (energy,) = sum_finish(STEPS + 1, 1)
    e_ref[0] = 2.0 * jnp.sum(energy)


def solution(mesh):
    n_cols = mesh.shape["col"]

    def local_fn(ham_blk, bounds, n_occ):
        rows_n, cols_n = ham_blk.shape
        n = cols_n * n_cols
        blk_n = n // PANELS
        f32 = jnp.float32
        return pl.pallas_call(
            lambda *refs: kernel(n, *refs),
            out_shape=(jax.ShapeDtypeStruct((rows_n, cols_n), f32), jax.ShapeDtypeStruct((1,), f32)),
            in_specs=[
                pl.BlockSpec(memory_space=pltpu.SMEM),
                pl.BlockSpec(memory_space=pltpu.SMEM),
                pl.BlockSpec(memory_space=pltpu.VMEM),
            ],
            out_specs=(pl.BlockSpec(memory_space=pltpu.VMEM), pl.BlockSpec(memory_space=pltpu.SMEM)),
            scratch_shapes=[
                pltpu.VMEM((2, PANELS, PANELS, blk_n, blk_n), f32),
                pltpu.VMEM((PANELS, blk_n, blk_n), f32),
                pltpu.VMEM((PANELS, blk_n, blk_n), f32),
                pltpu.VMEM((blk_n, blk_n), f32),
                pltpu.VMEM((STEPS + 2, PANELS, 3, 8, 128), f32),
                pltpu.VMEM((8, blk_n), f32),
                pltpu.VMEM((3, 8, 128), f32),
                pltpu.SemaphoreType.DMA((3, PANELS, SLOTS, 3)),
                pltpu.SemaphoreType.DMA((3, PANELS, SLOTS)),
                pltpu.SemaphoreType.DMA((STEPS + 2, PANELS)),
                pltpu.SemaphoreType.DMA((STEPS + 2, PANELS)),
                pltpu.SemaphoreType.DMA((PANELS,)),
                pltpu.SemaphoreType.DMA((PANELS,)),
            ],
            compiler_params=pltpu.CompilerParams(collective_id=0, has_side_effects=True, vmem_limit_bytes=60 << 20),
            name="purify",
        )(bounds, n_occ, ham_blk)

    spec_mat = P(("spin", "row"), "col")
    return jax.shard_map(local_fn, mesh=mesh, in_specs=(spec_mat, P("spin"), P("spin")), out_specs=(spec_mat, P("spin")), check_vma=False)
```

time: 695 us -> 217 us (0.31)
  waiting for transfers between devices: 423 us -> 0 us
  Pallas kernels: 0 us -> 210 us
  blocking collectives: 116 us -> 0 us
  matrix products: 114 us -> 0 us
  between operations: 26.3 us -> 3.02 us
  other arithmetic: 10.6 us -> 0 us
    all_gather x9 -> x0, waiting for transfers between devices: 421 us -> none  [the longest x3 173 us: local_fn(): x_rows = lax.all_gather(density, 'col', axis=1, tiled=True)]
    pallas_call x0 -> x1, Pallas kernels: none -> 210 us  [local_fn(): pl.pallas_call(lambda *refs: kernel(n, *refs), out_shape=(jax.ShapeDtypeS...]
    psum x5 -> x0, blocking collectives: 116 us -> none  [the longest x3 68.3 us: local_fn(): traces = lax.psum(part_sums, ('row', 'col'))]
    dot_general x6 -> x0, matrix products: 114 us -> none  [the longest x3 57.3 us: local_fn(): jnp.dot(x_rows, x_cols, precision=highest, preferred_element_type=jnp.flo...]
  transfers between devices with their start and end apart: 9 -> 0, of which waited for: 9 -> 0; matrix products, arithmetic and copies ran while one was open for 1% -> 0% of each run, Pallas kernels for 0% -> 0%
where the time goes in v2:
time: 217 us
  Pallas kernels  210 us (97%)
  local copies, waits for them, and re-layouts  3.08 us (1%)
  between operations  3.02 us (1%)
    pallas_call x1, Pallas kernels, local_fn(): pl.pallas_call(lambda *refs: kernel(n, *refs), out_shape=(jax.ShapeDtypeS...  210 us

profile of v2, /device:TPU:0, one launch (start us, length us, event | category | flops | bytes accessed | tf_op | source)
XLA Modules:
  0.0 216.5 jit_solution(3201902030288116591)
XLA Ops:
  1.3 210.4 %purify.1 = (f32[1024,512]{1,0:T(8,128)}, f32[1]{0:T(128)}) custom-call(f32[2]{0:T(128)} %refs_0_.1, s32[1]{0:T(128)S(6)} %copy.7.refs_1_, f32[1024,512]{1,0:T(8,128)} %refs_2_.1), custom_call_target="tpu_custom_call" | custom-call | tf_op jit(solution)/shard_map/purify/pallas_call | solution.py:484
  211.7 3.1 %copy.8 = f32[1024,512]{1,0:T(8,128)} copy(f32[1024,512]{1,0:T(8,128)} %get-tuple-element.4) | data formatting | bytes 4194304

commit v3 on v2

--- a/solution.py
+++ b/solution.py
@@ -22,7 +22,7 @@
 
 
 def pick(index, values):
-    return sum(flag(index == k) * v for k, v in enumerate(values) if v)
+    return sum(flag(index == k) * v for k, v in enumerate(values) if not (isinstance(v, int) and v == 0))
 
 
 def half(val, by=2):
@@ -153,29 +153,38 @@
                 def _():
                     act(self.copy(at, t, 1))
 
-        def arrive(self, mask, at, t):
+        def forward_any(self, k, masks, at, t, act):
+            for mask in (XN, YN, DIAG):
+                if mask in masks:
+
+                    @pl.when(k == masks.index(mask))
+                    def _():
+                        self.forward(mask, at, t, act)
+
+        def arrive(self, k, masks, at, t):
             self.copy(at, t, 0).wait_recv()
-            self.forward(mask, at, t, lambda copy: copy.start())
+            self.forward_any(k, masks, at, t, lambda copy: copy.start())
 
         def at(self, src, t):
             return (src.q, *self.place(src, t))
 
-        def each(self, jobs, first=0, last=SLOTS):
-            @pl.loop(0, last - first)
+        def each(self, masks, body, first=0, last=SLOTS):
+            srcs = [mask if isinstance(mask, Source) else sources[mask] for mask in masks]
+            many = len(srcs)
+
+            @pl.loop(0, (last - first) * many)
             def _(i):
-                t = i + first
-                for mask, body in jobs:
-                    src = mask if isinstance(mask, Source) else sources[mask]
-
-                    @pl.when(t < self.count(src))
-                    def _():
-                        body(mask, self.at(src, t), t)
+                t, k = first + half(i, many), part(i, many)
+                src = srcs[0] if many == 1 else Source(*(pick(k, vals) for vals in zip(*(src.fields for src in srcs))))
+
+                @pl.when(t < self.count(src))
+                def _():
+                    body(k, self.at(src, t), t)
 
         def drain(self):
-            def fwd(mask, at, t):
-                self.forward(mask, at, t, lambda copy: copy.wait_send())
-
-            self.each([(0, lambda mask, at, t: self.own(at, t, lambda copy: copy.wait_send()))] + [(mask, fwd) for mask in (XN, YN, DIAG)])
+            self.each((0,), lambda k, at, t: self.own(at, t, lambda copy: copy.wait_send()))
+            far = (XN, YN, DIAG)
+            self.each(far, lambda k, at, t: self.forward_any(k, far, at, t, lambda copy: copy.wait_send()))
 
     def part_copy(rnd, src, mask):
         return pltpu.make_async_remote_copy(
@@ -226,7 +235,7 @@
         return h_ref.at[span(row - 4 * y), span(col - 2 * j)]
 
     hx = Exchange(0, 1, h_place, lambda src: src.h_count, h_src)
-    hx.each([(0, lambda mask, at, t: hx.own(at, t, lambda copy: copy.start()))])
+    hx.each((0,), lambda k, at, t: hx.own(at, t, lambda copy: copy.start()))
 
     rows_n, cols_n = h_ref.shape
     mu_part = jnp.zeros((8, 128), jnp.float32)
@@ -247,9 +256,9 @@
     coef[1:2, :] = jnp.broadcast_to(mu, (1, blk_n))
     coef[2:3, :] = jnp.broadcast_to(jnp.full((1, 1), occ / n, jnp.float32), (1, blk_n))
 
-    def first_x(mask, at):
+    def first_x(own, at):
         _, row, col = at
-        blk = h_src(row, col)[...] if mask == 0 else buf[1, row, col]
+        blk = h_src(row, col)[...] if own else buf[1, row, col]
         diag = eye * (row == col).astype(jnp.float32)
         val = coef[0:1, :] * (coef[1:2, :] * diag - blk) + coef[2:3, :] * diag
         buf[0, row, col] = val
@@ -276,28 +285,41 @@
                 buf[buf_id, col, row] = blk.T
             x2row[row] += dot(buf[buf_id, me, col], blk, NT)
 
-    def h_take(mask, at, t):
-        if mask != 0:
-            hx.arrive(mask, at, t)
-        first_x(mask, at)
-
-    def h_use(mask, at, t):
+    def h_take(masks):
+        def body(k, at, t):
+            hx.arrive(k, masks, at, t)
+            first_x(False, at)
+
+        return body
+
+    def h_use(k, at, t):
         use(0, *at[1:], False)
 
-    def h_both(mask, at, t):
-        h_take(mask, at, t)
-        h_use(mask, at, t)
+    @pl.loop(0, 4)
+    def _(k):
+        first_x(True, (me, 4 * y + k, me))
+
+    hx.each((0,), lambda k, at, t: first_x(True, at))
+    hx.each((PARTNER,), h_take((PARTNER,)))
 
     early = [sources[k] * on + sources[XN + k] * (1 - on) for k in (0, PARTNER)]
     late = [sources[k] * (1 - on) + sources[XN + k] * on for k in (0, PARTNER)]
-    @pl.loop(0, 4)
-    def _(k):
-        first_x(0, (me, 4 * y + k, me))
-
-    hx.each([(mask, h_take) for mask in (0, PARTNER)])
-    hx.each([(mask, h_take) for mask in (XN, YN, XN + 2, YN + 2)] + [(src, h_use) for src in early])
-    hx.each([(src, h_use) for src in late + [sources[YN], sources[YN + 2]]] + [(DIAG, h_take)])
-    hx.each([(DIAG, h_use), (DIAG + 2, h_both)])
+    near = (XN, YN, XN + 2, YN + 2)
+
+    @pl.loop(0, SLOTS)
+    def _(t):
+        hx.each(near, h_take(near), t, t + 1)
+        hx.each(early, h_use, t, t + 1)
+
+    @pl.loop(0, SLOTS)
+    def _(t):
+        hx.each(late + [sources[YN], sources[YN + 2]], h_use, t, t + 1)
+        hx.each((DIAG,), h_take((DIAG,)), t, t + 1)
+
+    @pl.loop(0, SLOTS)
+    def _(t):
+        hx.each((DIAG + 2,), h_take((DIAG + 2,)), t, t + 1)
+        hx.each((DIAG, DIAG + 2), h_use, t, t + 1)
 
     def product(old, col):
         tot = dot(x2row[0], buf[old, 0, col], NN)
@@ -352,27 +374,34 @@
 
         clear()
 
-        def x_use(mask, at, t):
+        def x_use(k, at, t):
             use(new, *at[1:], True)
 
-        def x_take(mask, at, t):
-            ex.arrive(mask, at, t)
-            _, row, col = at
-
-            @pl.when(col == me)
-            def _():
-                buf[new, me, row] = buf[new, row, col].T
-
-        def x_both(mask, at, t):
-            ex.arrive(mask, at, t)
-            x_use(mask, at, t)
+        def x_take(masks):
+            def body(k, at, t):
+                ex.arrive(k, masks, at, t)
+                _, row, col = at
+
+                @pl.when(col == me)
+                def _():
+                    buf[new, me, row] = buf[new, row, col].T
+
+            return body
+
+        def x_both(masks):
+            def body(k, at, t):
+                ex.arrive(k, masks, at, t)
+                use(new, *at[1:], True)
+
+            return body
 
         near = (PARTNER, XN, YN, XN + 2, YN + 2)
-        ex.each([(0, x_use)])
-        ex.each([(mask, x_take) for mask in near], 0, 2)
-        ex.each([(mask, x_use) for mask in near], 0, 2)
-        ex.each([(mask, x_both) for mask in near], 2, SLOTS)
-        ex.each([(mask, x_both) for mask in (DIAG, DIAG + 2)])
+        far = (DIAG, DIAG + 2)
+        ex.each((0,), x_use)
+        ex.each(near, x_take(near), 0, 2)
+        ex.each(near, x_use, 0, 2)
+        ex.each(near, x_both(near), 2, SLOTS)
+        ex.each(far, x_both(far))
         before = ex
 
     old, end = (STEPS - 1) % 2, STEPS % 2

time: 217 us -> 220 us (1.014)
  Pallas kernels: 210 us -> 214 us
    pallas_call x1, Pallas kernels: 210 us -> 214 us  [local_fn(): pl.pallas_call(lambda *refs: kernel(n, *refs), out_shape=(jax.ShapeDtypeS...]
where the time goes in v3:
time: 220 us
  Pallas kernels  214 us (97%)
  local copies, waits for them, and re-layouts  3.08 us (1%)
  between operations  3.02 us (1%)
    pallas_call x1, Pallas kernels, local_fn(): pl.pallas_call(lambda *refs: kernel(n, *refs), out_shape=(jax.ShapeDtypeS...  214 us

profile of v3, /device:TPU:0, one launch (start us, length us, event | category | flops | bytes accessed | tf_op | source)
XLA Modules:
  0.0 220.1 jit_solution(12860815861116699422)
XLA Ops:
  1.3 213.9 %purify.1 = (f32[1024,512]{1,0:T(8,128)}, f32[1]{0:T(128)}) custom-call(f32[2]{0:T(128)} %refs_0_.1, s32[1]{0:T(128)S(6)} %copy.7.refs_1_, f32[1024,512]{1,0:T(8,128)} %refs_2_.1), custom_call_target="tpu_custom_call" | custom-call | tf_op jit(solution)/shard_map/purify/pallas_call | solution.py:513
  215.2 3.1 %copy.8 = f32[1024,512]{1,0:T(8,128)} copy(f32[1024,512]{1,0:T(8,128)} %get-tuple-element.4) | data formatting | bytes 4194304

commit v4 on v3

--- a/solution.py
+++ b/solution.py
@@ -123,20 +123,20 @@
             self.own_src = own_src or (lambda row, col: buf.at[buf_id, row, col])
 
         def copy(self, at, t, way, src=None):
-            q, row, col = at
+            q, row, col, _ = at
             block = buf.at[self.buf_id, row, col]
             return pltpu.make_async_remote_copy(
                 src_ref=block if src is None else src,
                 dst_ref=block,
-                send_sem=send_sem.at[self.rnd, q, t, way],
-                recv_sem=recv_sem.at[self.rnd, q, t],
+                send_sem=send_sem.at[self.rnd % 2, q, t, way],
+                recv_sem=recv_sem.at[self.rnd % 2, q, t],
                 device_id=devices[(PARTNER, XN, YN)[way]],
                 device_id_type=MESH,
             )
 
         def own(self, at, t, act):
             for way in range(3):
-                act(self.copy(at, t, way, self.own_src(*at[1:])))
+                act(self.copy(at, t, way, self.own_src(*at[1:3])))
 
         def forward(self, mask, at, t, act):
             if mask in (XN, YN, DIAG):
@@ -166,7 +166,7 @@
             self.forward_any(k, masks, at, t, lambda copy: copy.start())
 
         def at(self, src, t):
-            return (src.q, *self.place(src, t))
+            return (src.q, *self.place(src, t), src)
 
         def each(self, masks, body, first=0, last=SLOTS):
             srcs = [mask if isinstance(mask, Source) else sources[mask] for mask in masks]
@@ -257,7 +257,7 @@
     coef[2:3, :] = jnp.broadcast_to(jnp.full((1, 1), occ / n, jnp.float32), (1, blk_n))
 
     def first_x(own, at):
-        _, row, col = at
+        _, row, col = at[:3]
         blk = h_src(row, col)[...] if own else buf[1, row, col]
         diag = eye * (row == col).astype(jnp.float32)
         val = coef[0:1, :] * (coef[1:2, :] * diag - blk) + coef[2:3, :] * diag
@@ -275,15 +275,29 @@
         def _():
             hrow[row] = blk.T
 
-    def use(buf_id, row, col, turn):
-        blk = buf[buf_id, row, col]
-        x2row[col] += dot(buf[buf_id, me, row], blk, NN)
-
-        @pl.when(row != col)
-        def _():
-            if turn:
-                buf[buf_id, col, row] = blk.T
-            x2row[row] += dot(buf[buf_id, me, col], blk, NT)
+    def use(b, row, col):
+        blk = buf[b, row, col]
+        x2row[col] += dot(buf[b, me, row], blk, NN)
+        x2row[row] += dot(buf[b, me, col], blk, NT)
+        buf[b, col, row] = blk.T
+
+    def use_pair(b, row, col):
+        blk = [buf[b, row, k] for k in col]
+        left = buf[b, me, row]
+        right = [buf[b, me, k] for k in col]
+        for k in range(2):
+            x2row[col[k]] += dot(left, blk[k], NN)
+        x2row[row] += dot(right[0], blk[0], NT) + dot(right[1], blk[1], NT)
+        for k in range(2):
+            buf[b, col[k], row] = blk[k].T
+
+    def use_diag(b, row, col):
+        blk, mid = buf[b, row, col], buf[b, row, row]
+        left = buf[b, me, row]
+        right = buf[b, me, col]
+        x2row[col] += dot(left, blk, NN)
+        x2row[row] += dot(right, blk, NT) + dot(left, mid, NN)
+        buf[b, col, row] = blk.T
 
     def h_take(masks):
         def body(k, at, t):
@@ -292,8 +306,11 @@
 
         return body
 
-    def h_use(k, at, t):
-        use(0, *at[1:], False)
+    def h_unit(col, kind):
+        cross = half(kind)
+        first = 4 * flip(half(col, 4), cross) + (1 - cross) * 2 * kind + cross * flip(part(col), part(kind))
+        second = first + 1 + cross
+        x2row[col] += dot(buf[0, me, first], buf[0, first, col], NN) + dot(buf[0, me, second], buf[0, second, col], NN)
 
     @pl.loop(0, 4)
     def _(k):
@@ -302,24 +319,30 @@
     hx.each((0,), lambda k, at, t: first_x(True, at))
     hx.each((PARTNER,), h_take((PARTNER,)))
 
-    early = [sources[k] * on + sources[XN + k] * (1 - on) for k in (0, PARTNER)]
-    late = [sources[k] * (1 - on) + sources[XN + k] * on for k in (0, PARTNER)]
     near = (XN, YN, XN + 2, YN + 2)
-
-    @pl.loop(0, SLOTS)
-    def _(t):
-        hx.each(near, h_take(near), t, t + 1)
-        hx.each(early, h_use, t, t + 1)
-
-    @pl.loop(0, SLOTS)
-    def _(t):
-        hx.each(late + [sources[YN], sources[YN + 2]], h_use, t, t + 1)
-        hx.each((DIAG,), h_take((DIAG,)), t, t + 1)
-
-    @pl.loop(0, SLOTS)
-    def _(t):
-        hx.each((DIAG + 2,), h_take((DIAG + 2,)), t, t + 1)
-        hx.each((DIAG, DIAG + 2), h_use, t, t + 1)
+    far = (DIAG, DIAG + 2)
+    off = 1 - on
+    hx.each(near, h_take(near), 0, 1)
+
+    @pl.loop(0, 4 + 4 * on)
+    def _(i):
+        h_unit(on * (4 * y + half(i)) + off * (4 - 4 * y + i), on * part(i) + off * (2 + y))
+
+    hx.each(near, h_take(near), 1, SLOTS)
+
+    @pl.loop(0, 16)
+    def _(i):
+        h_unit(on * (4 * flip(y, half(i, 8)) + half(part(i, 8))) + off * half(i), on * 2 + part(i))
+
+    @pl.loop(0, 4 * off)
+    def _(i):
+        h_unit(4 * y + i, 2 + y)
+
+    hx.each(far, h_take(far))
+
+    @pl.loop(0, 8)
+    def _(i):
+        h_unit(on * (4 - 4 * y + half(i)) + off * i, on * part(i) + off * (3 - y))
 
     def product(old, col):
         tot = dot(x2row[0], buf[old, 0, col], NN)
@@ -374,13 +397,10 @@
 
         clear()
 
-        def x_use(k, at, t):
-            use(new, *at[1:], True)
-
         def x_take(masks):
             def body(k, at, t):
                 ex.arrive(k, masks, at, t)
-                _, row, col = at
+                _, row, col = at[:3]
 
                 @pl.when(col == me)
                 def _():
@@ -388,20 +408,31 @@
 
             return body
 
-        def x_both(masks):
-            def body(k, at, t):
-                ex.arrive(k, masks, at, t)
-                use(new, *at[1:], True)
-
-            return body
+        def x_first(k, at, t):
+            src = at[3]
+            use_pair(new, at[1], (at[2], x_place(src, 1)[1]))
+
+        def x_second(k, at, t):
+            use_diag(new, at[1], at[2])
+
+        def x_last(k, at, t):
+            use(new, at[1], at[2])
 
         near = (PARTNER, XN, YN, XN + 2, YN + 2)
         far = (DIAG, DIAG + 2)
-        ex.each((0,), x_use)
+        ex.each((0,), x_first, 0, 1)
         ex.each(near, x_take(near), 0, 2)
-        ex.each(near, x_use, 0, 2)
-        ex.each(near, x_both(near), 2, SLOTS)
-        ex.each(far, x_both(far))
+        ex.each(near, x_first, 0, 1)
+        ex.each(near, x_take(near), 2, 4)
+        ex.each((0, *near), x_second, 2, 3)
+        ex.each(near, x_take(near), 4, 5)
+        ex.each((0, *near), x_last, 4, 5)
+        ex.each(far, x_take(far), 0, 2)
+        ex.each(far, x_first, 0, 1)
+        ex.each(far, x_take(far), 2, 4)
+        ex.each(far, x_second, 2, 3)
+        ex.each(far, x_take(far), 4, 5)
+        ex.each(far, x_last, 4, 5)
         before = ex
 
     old, end = (STEPS - 1) % 2, STEPS % 2
@@ -527,8 +558,8 @@
                 pltpu.VMEM((STEPS + 2, PANELS, 3, 8, 128), f32),
                 pltpu.VMEM((8, blk_n), f32),
                 pltpu.VMEM((3, 8, 128), f32),
-                pltpu.SemaphoreType.DMA((3, PANELS, SLOTS, 3)),
-                pltpu.SemaphoreType.DMA((3, PANELS, SLOTS)),
+                pltpu.SemaphoreType.DMA((2, PANELS, SLOTS, 3)),
+                pltpu.SemaphoreType.DMA((2, PANELS, SLOTS)),
                 pltpu.SemaphoreType.DMA((STEPS + 2, PANELS)),
                 pltpu.SemaphoreType.DMA((STEPS + 2, PANELS)),
                 pltpu.SemaphoreType.DMA((PANELS,)),

time: 220 us -> 214 us (0.973)
  Pallas kernels: 214 us -> 208 us
    pallas_call x1, Pallas kernels: 214 us -> 208 us  [local_fn(): pl.pallas_call(lambda *refs: kernel(n, *refs), out_shape=(jax.ShapeDtypeS...]
where the time goes in v4:
time: 214 us
  Pallas kernels  208 us (97%)
  local copies, waits for them, and re-layouts  3.08 us (1%)
  between operations  3.02 us (1%)
    pallas_call x1, Pallas kernels, local_fn(): pl.pallas_call(lambda *refs: kernel(n, *refs), out_shape=(jax.ShapeDtypeS...  208 us

profile of v4, /device:TPU:0, one launch (start us, length us, event | category | flops | bytes accessed | tf_op | source)
XLA Modules:
  0.0 213.9 jit_solution(6486576415726499859)
XLA Ops:
  1.3 207.8 %purify.1 = (f32[1024,512]{1,0:T(8,128)}, f32[1]{0:T(128)}) custom-call(f32[2]{0:T(128)} %refs_0_.1, s32[1]{0:T(128)S(6)} %copy.7.refs_1_, f32[1024,512]{1,0:T(8,128)} %refs_2_.1), custom_call_target="tpu_custom_call" | custom-call | tf_op jit(solution)/shard_map/purify/pallas_call | solution.py:544
  209.0 3.1 %copy.8 = f32[1024,512]{1,0:T(8,128)} copy(f32[1024,512]{1,0:T(8,128)} %get-tuple-element.4) | data formatting | bytes 4194304

commit v5 on v4

--- a/solution.py
+++ b/solution.py
@@ -8,6 +8,7 @@
 STEPS = 3
 PANELS = 8
 SLOTS = 5
+CORNERS = 2
 MESH = pl.DeviceIdType.MESH
 NN = (((1,), (0,)), ((), ()))
 NT = (((1,), (1,)), ((), ()))
@@ -49,10 +50,10 @@
     x, y, c = panel_bits(q)
     if x == y:
         local = {
-            (0, 0): ((1, 1), (1, 0), (3, 0), (0, 0), (2, 0)),
-            (0, 1): ((3, 1), (3, 0), (1, 0), (1, 1), (2, 0)),
-            (1, 0): ((0, 0), (1, 0), (2, 0), (3, 0), (1, 1)),
-            (1, 1): ((2, 0), (3, 0), (1, 0), (3, 1), (1, 1)),
+            (0, 0): ((1, 0), (3, 0), (2, 0), (0, 0), (1, 1)),
+            (0, 1): ((3, 0), (1, 0), (1, 1), (2, 0), (3, 1)),
+            (1, 0): ((1, 0), (2, 0), (3, 0), (0, 0), (1, 1)),
+            (1, 1): ((3, 0), (1, 0), (1, 1), (2, 0), (3, 1)),
         }[x, c]
     else:
         local = tuple((2 * k + (b + y) % 2, b) for b in range(2) for k in range(2))
@@ -122,11 +123,11 @@
             self.rnd, self.buf_id, self.place, self.count = rnd, buf_id, place, count
             self.own_src = own_src or (lambda row, col: buf.at[buf_id, row, col])
 
-        def copy(self, at, t, way, src=None):
+        def copy(self, at, t, way, view, src=None):
             q, row, col, _ = at
-            block = buf.at[self.buf_id, row, col]
+            block = view(buf.at[self.buf_id, row, col])
             return pltpu.make_async_remote_copy(
-                src_ref=block if src is None else src,
+                src_ref=block if src is None else view(src),
                 dst_ref=block,
                 send_sem=send_sem.at[self.rnd % 2, q, t, way],
                 recv_sem=recv_sem.at[self.rnd % 2, q, t],
@@ -134,24 +135,41 @@
                 device_id_type=MESH,
             )
 
+        def pieces(self, at, t, body):
+            mid = blk_n // 2
+
+            @pl.when(at[1] != at[2])
+            def _():
+                body(t, lambda ref: ref, flag(t == 0) + flag(t == 2))
+
+            @pl.when(at[1] == at[2])
+            def _():
+                body(t, lambda ref: ref.at[pl.ds(0, mid), :], jnp.int32(0))
+                body(t + CORNERS, lambda ref: ref.at[pl.ds(mid, mid), pl.ds(mid, mid)], flag(t == 4))
+
         def own(self, at, t, act):
-            for way in range(3):
-                act(self.copy(at, t, way, self.own_src(*at[1:3])))
+            def body(slot, view, x_way):
+                for way in range(3):
+                    act(self.copy(at, slot, way, view, self.own_src(*at[1:3])))
+
+            self.pieces(at, t, body)
 
         def forward(self, mask, at, t, act):
-            if mask in (XN, YN, DIAG):
-                act(self.copy(at, t, 0))
-            if mask == XN:
-
-                @pl.when(part(t) + flag(t == 4) * y == 0)
-                def _():
-                    act(self.copy(at, t, 2))
-
-            if mask == YN:
-
-                @pl.when(part(t) + flag(t == 4) * (1 - y) == 1)
-                def _():
-                    act(self.copy(at, t, 1))
+            def body(slot, view, x_way):
+                act(self.copy(at, slot, 0, view))
+                if mask == XN:
+
+                    @pl.when(x_way == 1)
+                    def _():
+                        act(self.copy(at, slot, 2, view))
+
+                if mask == YN:
+
+                    @pl.when(x_way == 0)
+                    def _():
+                        act(self.copy(at, slot, 1, view))
+
+            self.pieces(at, t, body)
 
         def forward_any(self, k, masks, at, t, act):
             for mask in (XN, YN, DIAG):
@@ -162,8 +180,14 @@
                         self.forward(mask, at, t, act)
 
         def arrive(self, k, masks, at, t):
-            self.copy(at, t, 0).wait_recv()
+            self.pieces(at, t, lambda slot, view, x_way: self.copy(at, slot, 0, view).wait_recv())
             self.forward_any(k, masks, at, t, lambda copy: copy.start())
+            mid = blk_n // 2
+
+            @pl.when(at[1] == at[2])
+            def _():
+                block = buf.at[self.buf_id, at[1], at[2]]
+                block[mid:, :mid] = block[:mid, mid:].T
 
         def at(self, src, t):
             return (src.q, *self.place(src, t), src)
@@ -198,7 +222,7 @@
 
     def sum_start(rnd, vals):
         for k, val in enumerate(vals):
-            parts[rnd, me, k] = val
+            parts[rnd, me, k : k + 1] = jnp.sum(val, axis=0, keepdims=True)
         for mask in range(1, 8):
             part_copy(rnd, me, mask).start()
 
@@ -207,13 +231,10 @@
             part_copy(rnd, sources[mask].q, mask).wait_recv()
         for mask in range(1, 8):
             part_copy(rnd, me, mask).wait_send()
-        out = []
-        for k in range(count):
-            tot = parts[rnd, 0, k]
-            for q in range(1, PANELS):
-                tot = tot + parts[rnd, q, k]
-            out.append(jnp.sum(jnp.sum(tot, axis=1, keepdims=True), axis=0, keepdims=True))
-        return out
+        tot = parts[rnd, 0]
+        for q in range(1, PANELS):
+            tot = tot + parts[rnd, q]
+        return [jnp.sum(tot[k : k + 1], axis=1, keepdims=True) for k in range(count)]
 
     def fold(val):
         rows, cols = val.shape
@@ -555,17 +576,17 @@
                 pltpu.VMEM((PANELS, blk_n, blk_n), f32),
                 pltpu.VMEM((PANELS, blk_n, blk_n), f32),
                 pltpu.VMEM((blk_n, blk_n), f32),
-                pltpu.VMEM((STEPS + 2, PANELS, 3, 8, 128), f32),
+                pltpu.VMEM((STEPS + 2, PANELS, 8, 128), f32),
                 pltpu.VMEM((8, blk_n), f32),
                 pltpu.VMEM((3, 8, 128), f32),
-                pltpu.SemaphoreType.DMA((2, PANELS, SLOTS, 3)),
-                pltpu.SemaphoreType.DMA((2, PANELS, SLOTS)),
+                pltpu.SemaphoreType.DMA((2, PANELS, SLOTS + CORNERS, 3)),
+                pltpu.SemaphoreType.DMA((2, PANELS, SLOTS + CORNERS)),
                 pltpu.SemaphoreType.DMA((STEPS + 2, PANELS)),
                 pltpu.SemaphoreType.DMA((STEPS + 2, PANELS)),
                 pltpu.SemaphoreType.DMA((PANELS,)),
                 pltpu.SemaphoreType.DMA((PANELS,)),
             ],
-            compiler_params=pltpu.CompilerParams(collective_id=0, has_side_effects=True, vmem_limit_bytes=60 << 20),
+            compiler_params=pltpu.CompilerParams(collective_id=0, has_side_effects=True, vmem_limit_bytes=48 << 20),
             name="purify",
         )(bounds, n_occ, ham_blk)
 

time: 214 us -> 208 us (0.972)
  Pallas kernels: 208 us -> 201 us
    pallas_call x1, Pallas kernels: 208 us -> 201 us  [local_fn(): pl.pallas_call(lambda *refs: kernel(n, *refs), out_shape=(jax.ShapeDtypeS...]
where the time goes in v5:
time: 208 us
  Pallas kernels  201 us (97%)
  local copies, waits for them, and re-layouts  3.56 us (2%)
  between operations  3.06 us (1%)
    pallas_call x1, Pallas kernels, local_fn(): pl.pallas_call(lambda *refs: kernel(n, *refs), out_shape=(jax.ShapeDtypeS...  201 us

profile of v5, /device:TPU:0, one launch (start us, length us, event | category | flops | bytes accessed | tf_op | source)
XLA Modules:
  0.0 207.8 jit_solution(8488716243801752255)
XLA Ops:
  1.3 0.0 copy-start
  1.3 1.6 copy-done
  2.9 0.0 copy-start.1
  2.9 0.7 copy-done.1
  3.5 201.2 %purify.1 = (f32[1024,512]{1,0:T(8,128)S(1)}, f32[1]{0:T(128)}) custom-call(f32[2]{0:T(128)S(1)} %copy-done.1, s32[1]{0:T(128)S(6)} %copy.7.refs_1_, f32[1024,512]{1,0:T(8,128)S(1)} %copy-done), custom_call_target="tpu_custom_call" | custom-call | tf_op jit(solution)/shard_map/purify/pallas_call | solution.py:565
  204.8 1.3 copy.8
Async XLA Ops:
  1.3 1.6 copy-start
  2.9 0.7 copy-start.1

commit v6 on v5

--- a/solution.py
+++ b/solution.py
@@ -65,7 +65,7 @@
     return tuple(q ^ m for m in (4 + 2 * x, 1 + 2 * y, 5 + 2 * y, 0, 2, 7 - 2 * y))
 
 
-def kernel(n, bounds, n_occ, h_ref, out_ref, e_ref, buf, hrow, x2row, acc, parts, coef, sums, send_sem, recv_sem, part_send, part_recv, last_send, last_recv):
+def kernel(n, bounds, n_occ, h_hbm, out_ref, e_ref, h_ref, h_sem, buf, hrow, x2row, acc, parts, coef, sums, send_sem, recv_sem, part_send, part_recv, last_send, last_recv):
     blk_n = n // PANELS
     y = lax.axis_index("row")
     j = lax.axis_index("col")
@@ -108,15 +108,22 @@
     def x_place(src, t):
         return src.q, part(lax.div(src.x_pack, pick(t, [8**k for k in range(SLOTS + 1)])), 8)
 
+    def x_at(src, t):
+        return src.q, src.q, part(half(src.x_pack, 8**t), 8), src
+
     devices = [device(jnp.int32(mask)) for mask in range(8)]
     sources = [source(mask) for mask in range(8)]
 
     PARTNER, XN, YN, DIAG = 2, 4, 1, 5
+
+    h_in = pltpu.make_async_copy(h_hbm, h_ref, h_sem)
+    h_in.start()
 
     barrier = pltpu.get_barrier_semaphore()
     for mask in range(1, 8):
         pl.semaphore_signal(barrier, inc=1, device_id=devices[mask], device_id_type=MESH)
     pl.semaphore_wait(barrier, 7)
+    h_in.wait()
 
     class Exchange:
         def __init__(self, rnd, buf_id, place, count, own_src=None):
@@ -189,6 +196,24 @@
                 block = buf.at[self.buf_id, at[1], at[2]]
                 block[mid:, :mid] = block[:mid, mid:].T
 
+        def take(self, mask, at, t):
+            mid = blk_n // 2
+            views = [(t, lambda ref: ref)]
+            if t == 3:
+                views = [(t, lambda ref: ref.at[pl.ds(0, mid), :]), (t + CORNERS, lambda ref: ref.at[pl.ds(mid, mid), pl.ds(mid, mid)])]
+            for slot, view in views:
+                self.copy(at, slot, 0, view).wait_recv()
+            for slot, view in views:
+                if mask in (XN, YN, DIAG):
+                    self.copy(at, slot, 0, view).start()
+                if mask == XN and t in (0, 2):
+                    self.copy(at, slot, 2, view).start()
+                if mask == YN and t not in (0, 2):
+                    self.copy(at, slot, 1, view).start()
+            if t == 3:
+                block = buf.at[self.buf_id, at[1], at[2]]
+                block[mid:, :mid] = block[:mid, mid:].T
+
         def at(self, src, t):
             return (src.q, *self.place(src, t), src)
 
@@ -349,21 +374,39 @@
     def _(i):
         h_unit(on * (4 * y + half(i)) + off * (4 - 4 * y + i), on * part(i) + off * (2 + y))
 
-    hx.each(near, h_take(near), 1, SLOTS)
+    hx.each(near, h_take(near), 1, 3)
+
+    @pl.loop(0, 4 * off)
+    def _(i):
+        h_unit(4 * y + i, 1 - half(i))
+
+    hx.each(near, h_take(near), 3, SLOTS)
 
     @pl.loop(0, 16)
     def _(i):
-        h_unit(on * (4 * flip(y, half(i, 8)) + half(part(i, 8))) + off * half(i), on * 2 + part(i))
+        col, kind = on * (4 * flip(y, half(i, 8)) + half(part(i, 8))) + off * half(i), on * 2 + part(i)
+
+        @pl.when(on + flag(half(col, 4) != y) + flag(kind == half(part(col, 4))) > 0)
+        def _():
+            h_unit(col, kind)
 
     @pl.loop(0, 4 * off)
     def _(i):
         h_unit(4 * y + i, 2 + y)
 
-    hx.each(far, h_take(far))
-
-    @pl.loop(0, 8)
+    hx.each(far, h_take(far), 0, 2)
+
+    @pl.loop(0, 4 * off)
     def _(i):
-        h_unit(on * (4 - 4 * y + half(i)) + off * i, on * part(i) + off * (3 - y))
+        late_half = half(i)
+        h_unit(4 * flip(y, late_half) + 2 * part(i) + late_half * (1 - y), 3 - y)
+
+    hx.each(far, h_take(far), 2, SLOTS)
+
+    @pl.loop(0, 4 + 4 * on)
+    def _(i):
+        late_half = half(i)
+        h_unit(on * (4 - 4 * y + half(i)) + off * (4 * flip(y, late_half) + 2 * part(i) + 1 - late_half * (1 - y)), on * part(i) + off * (3 - y))
 
     def product(old, col):
         tot = dot(x2row[0], buf[old, 0, col], NN)
@@ -418,16 +461,24 @@
 
         clear()
 
-        def x_take(masks):
-            def body(k, at, t):
-                ex.arrive(k, masks, at, t)
-                _, row, col = at[:3]
-
-                @pl.when(col == me)
-                def _():
-                    buf[new, me, row] = buf[new, row, col].T
-
-            return body
+        def x_take(masks, first, last):
+            for t in range(first, last):
+                for mask in masks:
+                    src = sources[mask]
+                    if t == 4:
+
+                        @pl.when(src.x_count == SLOTS)
+                        def _():
+                            ex.take(mask, x_at(src, t), t)
+
+                    else:
+                        at = x_at(src, t)
+                        ex.take(mask, at, t)
+                        if (mask, t) in ((XN, 0), (XN + 2, 0), (YN, 1), (YN + 2, 1)):
+
+                            @pl.when(at[2] == me)
+                            def _():
+                                buf[new, me, at[1]] = buf[new, at[1], at[2]].T
 
         def x_first(k, at, t):
             src = at[3]
@@ -442,17 +493,19 @@
         near = (PARTNER, XN, YN, XN + 2, YN + 2)
         far = (DIAG, DIAG + 2)
         ex.each((0,), x_first, 0, 1)
-        ex.each(near, x_take(near), 0, 2)
+        ex.each((0,), x_second, 2, 3)
+        ex.each((0,), x_last, 4, 5)
+        x_take(near, 0, 2)
         ex.each(near, x_first, 0, 1)
-        ex.each(near, x_take(near), 2, 4)
-        ex.each((0, *near), x_second, 2, 3)
-        ex.each(near, x_take(near), 4, 5)
-        ex.each((0, *near), x_last, 4, 5)
-        ex.each(far, x_take(far), 0, 2)
+        x_take(near, 2, 4)
+        ex.each(near, x_second, 2, 3)
+        x_take(near, 4, 5)
+        ex.each(near, x_last, 4, 5)
+        x_take(far, 0, 2)
         ex.each(far, x_first, 0, 1)
-        ex.each(far, x_take(far), 2, 4)
+        x_take(far, 2, 4)
         ex.each(far, x_second, 2, 3)
-        ex.each(far, x_take(far), 4, 5)
+        x_take(far, 4, 5)
         ex.each(far, x_last, 4, 5)
         before = ex
 
@@ -568,10 +621,12 @@
             in_specs=[
                 pl.BlockSpec(memory_space=pltpu.SMEM),
                 pl.BlockSpec(memory_space=pltpu.SMEM),
-                pl.BlockSpec(memory_space=pltpu.VMEM),
+                pl.BlockSpec(memory_space=pltpu.HBM),
             ],
             out_specs=(pl.BlockSpec(memory_space=pltpu.VMEM), pl.BlockSpec(memory_space=pltpu.SMEM)),
             scratch_shapes=[
+                pltpu.VMEM((rows_n, cols_n), f32),
+                pltpu.SemaphoreType.DMA,
                 pltpu.VMEM((2, PANELS, PANELS, blk_n, blk_n), f32),
                 pltpu.VMEM((PANELS, blk_n, blk_n), f32),
                 pltpu.VMEM((PANELS, blk_n, blk_n), f32),

time: 208 us -> 208 us (level)
  no operation moved by 1% of the time
where the time goes in v6:
time: 208 us
  Pallas kernels  201 us (97%)
  local copies, waits for them, and re-layouts  3.56 us (2%)
  between operations  3.06 us (1%)
    pallas_call x1, Pallas kernels, local_fn(): pl.pallas_call(lambda *refs: kernel(n, *refs), out_shape=(jax.ShapeDtypeS...  201 us

profile of v6, /device:TPU:0, one launch (start us, length us, event | category | flops | bytes accessed | tf_op | source)
XLA Modules:
  0.0 208.0 jit_solution(6074389937589925993)
XLA Ops:
  1.3 0.0 copy-start
  1.3 1.6 copy-done
  2.9 0.0 copy-start.1
  2.9 0.7 copy-done.1
  3.5 201.4 %purify.1 = (f32[1024,512]{1,0:T(8,128)S(1)}, f32[1]{0:T(128)}) custom-call(f32[2]{0:T(128)S(1)} %copy-done.1, s32[1]{0:T(128)S(6)} %copy.7.refs_1_, f32[1024,512]{1,0:T(8,128)S(1)} %copy-done), custom_call_target="tpu_custom_call" | custom-call | tf_op jit(solution)/shard_map/purify/pallas_call | solution.py:618
  204.9 1.3 copy.8
Async XLA Ops:
  1.3 1.6 copy-start
  2.9 0.7 copy-start.1

commit v7 on v6

--- a/solution.py
+++ b/solution.py
@@ -136,8 +136,8 @@
             return pltpu.make_async_remote_copy(
                 src_ref=block if src is None else view(src),
                 dst_ref=block,
-                send_sem=send_sem.at[self.rnd % 2, q, t, way],
-                recv_sem=recv_sem.at[self.rnd % 2, q, t],
+                send_sem=send_sem.at[self.rnd, q, t, way],
+                recv_sem=recv_sem.at[self.rnd, q, t],
                 device_id=devices[(PARTNER, XN, YN)[way]],
                 device_id_type=MESH,
             )
@@ -436,12 +436,13 @@
     def updated(old, col):
         return coef[0:1, :] * buf[old, me, col] + coef[1:2, :] * x2row[col] - coef[2:3, :] * acc[...]
 
-    before = hx
-    for step in range(STEPS - 1):
-        old, new = step % 2, (step + 1) % 2
-        before.drain()
+    hx.drain()
+
+    @pl.loop(0, STEPS - 1)
+    def _(step):
+        old, new = part(step), part(step + 1)
         traces(old, 1 + step)
-        ex = Exchange(1 + step, new, x_place, lambda src: src.x_count)
+        ex = Exchange(part(1 + step), new, x_place, lambda src: src.x_count)
 
         @pl.loop(0, SLOTS + 1)
         def _(t):
@@ -507,10 +508,9 @@
         ex.each(far, x_second, 2, 3)
         x_take(far, 4, 5)
         ex.each(far, x_last, 4, 5)
-        before = ex
+        ex.drain()
 
     old, end = (STEPS - 1) % 2, STEPS % 2
-    before.drain()
     traces(old, STEPS)
     sums[2] = jnp.zeros((8, 128), jnp.float32)
 

time: 208 us -> 208 us (level)
  no operation moved by 1% of the time
where the time goes in v7:
time: 208 us
  Pallas kernels  202 us (97%)
  local copies, waits for them, and re-layouts  3.56 us (2%)
  between operations  3.06 us (1%)
    pallas_call x1, Pallas kernels, local_fn(): pl.pallas_call(lambda *refs: kernel(n, *refs), out_shape=(jax.ShapeDtypeS...  202 us

profile of v7, /device:TPU:0, one launch (start us, length us, event | category | flops | bytes accessed | tf_op | source)
XLA Modules:
  0.0 208.1 jit_solution(17262914870242976908)
XLA Ops:
  1.3 0.0 copy-start
  1.3 1.6 copy-done
  2.9 0.0 copy-start.1
  2.9 0.7 copy-done.1
  3.5 201.5 %purify.1 = (f32[1024,512]{1,0:T(8,128)S(1)}, f32[1]{0:T(128)}) custom-call(f32[2]{0:T(128)S(1)} %copy-done.1, s32[1]{0:T(128)S(6)} %copy.7.refs_1_, f32[1024,512]{1,0:T(8,128)S(1)} %copy-done), custom_call_target="tpu_custom_call" | custom-call | tf_op jit(solution)/shard_map/purify/pallas_call | solution.py:618
  205.0 1.3 copy.8
Async XLA Ops:
  1.3 1.6 copy-start
  2.9 0.7 copy-start.1

commit v8 on v7

--- a/solution.py
+++ b/solution.py
@@ -126,8 +126,8 @@
     h_in.wait()
 
     class Exchange:
-        def __init__(self, rnd, buf_id, place, count, own_src=None):
-            self.rnd, self.buf_id, self.place, self.count = rnd, buf_id, place, count
+        def __init__(self, buf_id, place, count, own_src=None):
+            self.buf_id, self.place, self.count = buf_id, place, count
             self.own_src = own_src or (lambda row, col: buf.at[buf_id, row, col])
 
         def copy(self, at, t, way, view, src=None):
@@ -136,8 +136,8 @@
             return pltpu.make_async_remote_copy(
                 src_ref=block if src is None else view(src),
                 dst_ref=block,
-                send_sem=send_sem.at[self.rnd, q, t, way],
-                recv_sem=recv_sem.at[self.rnd, q, t],
+                send_sem=send_sem.at[q, t, way],
+                recv_sem=recv_sem.at[q, t],
                 device_id=devices[(PARTNER, XN, YN)[way]],
                 device_id_type=MESH,
             )
@@ -239,7 +239,7 @@
         return pltpu.make_async_remote_copy(
             src_ref=parts.at[rnd, src],
             dst_ref=parts.at[rnd, src],
-            send_sem=part_send.at[rnd, mask],
+            send_sem=part_send.at[mask],
             recv_sem=part_recv.at[rnd, src],
             device_id=devices[mask],
             device_id_type=MESH,
@@ -280,7 +280,7 @@
     def h_src(row, col):
         return h_ref.at[span(row - 4 * y), span(col - 2 * j)]
 
-    hx = Exchange(0, 1, h_place, lambda src: src.h_count, h_src)
+    hx = Exchange(1, h_place, lambda src: src.h_count, h_src)
     hx.each((0,), lambda k, at, t: hx.own(at, t, lambda copy: copy.start()))
 
     rows_n, cols_n = h_ref.shape
@@ -442,7 +442,7 @@
     def _(step):
         old, new = part(step), part(step + 1)
         traces(old, 1 + step)
-        ex = Exchange(part(1 + step), new, x_place, lambda src: src.x_count)
+        ex = Exchange(new, x_place, lambda src: src.x_count)
 
         @pl.loop(0, SLOTS + 1)
         def _(t):
@@ -634,9 +634,9 @@
                 pltpu.VMEM((STEPS + 2, PANELS, 8, 128), f32),
                 pltpu.VMEM((8, blk_n), f32),
                 pltpu.VMEM((3, 8, 128), f32),
-                pltpu.SemaphoreType.DMA((2, PANELS, SLOTS + CORNERS, 3)),
-                pltpu.SemaphoreType.DMA((2, PANELS, SLOTS + CORNERS)),
-                pltpu.SemaphoreType.DMA((STEPS + 2, PANELS)),
+                pltpu.SemaphoreType.DMA((PANELS, SLOTS + CORNERS, 3)),
+                pltpu.SemaphoreType.DMA((PANELS, SLOTS + CORNERS)),
+                pltpu.SemaphoreType.DMA((PANELS,)),
                 pltpu.SemaphoreType.DMA((STEPS + 2, PANELS)),
                 pltpu.SemaphoreType.DMA((PANELS,)),
                 pltpu.SemaphoreType.DMA((PANELS,)),

time: 208 us -> 206 us (level)
  Pallas kernels: 202 us -> 199 us
    pallas_call x1, Pallas kernels: 202 us -> 199 us  [local_fn(): pl.pallas_call(lambda *refs: kernel(n, *refs), out_shape=(jax.ShapeDtypeS...]
where the time goes in v8:
time: 206 us
  Pallas kernels  199 us (97%)
  local copies, waits for them, and re-layouts  3.56 us (2%)
  between operations  3.06 us (1%)
    pallas_call x1, Pallas kernels, local_fn(): pl.pallas_call(lambda *refs: kernel(n, *refs), out_shape=(jax.ShapeDtypeS...  199 us

profile of v8, /device:TPU:0, one launch (start us, length us, event | category | flops | bytes accessed | tf_op | source)
XLA Modules:
  0.0 205.8 jit_solution(10267198417039651474)
XLA Ops:
  1.3 0.0 copy-start
  1.3 1.6 copy-done
  2.9 0.0 copy-start.1
  2.9 0.7 copy-done.1
  3.5 199.2 %purify.1 = (f32[1024,512]{1,0:T(8,128)S(1)}, f32[1]{0:T(128)}) custom-call(f32[2]{0:T(128)S(1)} %copy-done.1, s32[1]{0:T(128)S(6)} %copy.7.refs_1_, f32[1024,512]{1,0:T(8,128)S(1)} %copy-done), custom_call_target="tpu_custom_call" | custom-call | tf_op jit(solution)/shard_map/purify/pallas_call | solution.py:618
  202.7 1.3 copy.8
Async XLA Ops:
  1.3 1.6 copy-start
  2.9 0.7 copy-start.1

commit v9 on v8

--- a/solution.py
+++ b/solution.py
@@ -115,6 +115,7 @@
     sources = [source(mask) for mask in range(8)]
 
     PARTNER, XN, YN, DIAG = 2, 4, 1, 5
+    FORWARD = {XN: 3, YN: 5, DIAG: 7}
 
     h_in = pltpu.make_async_copy(h_hbm, h_ref, h_sem)
     h_in.start()
@@ -130,13 +131,13 @@
             self.buf_id, self.place, self.count = buf_id, place, count
             self.own_src = own_src or (lambda row, col: buf.at[buf_id, row, col])
 
-        def copy(self, at, t, way, view, src=None):
+        def copy(self, at, t, way, view, src=None, sem=None):
             q, row, col, _ = at
             block = view(buf.at[self.buf_id, row, col])
             return pltpu.make_async_remote_copy(
                 src_ref=block if src is None else view(src),
                 dst_ref=block,
-                send_sem=send_sem.at[q, t, way],
+                send_sem=send_sem.at[way if sem is None else sem, t],
                 recv_sem=recv_sem.at[q, t],
                 device_id=devices[(PARTNER, XN, YN)[way]],
                 device_id_type=MESH,
@@ -163,18 +164,18 @@
 
         def forward(self, mask, at, t, act):
             def body(slot, view, x_way):
-                act(self.copy(at, slot, 0, view))
+                act(self.copy(at, slot, 0, view, sem=FORWARD[mask]))
                 if mask == XN:
 
                     @pl.when(x_way == 1)
                     def _():
-                        act(self.copy(at, slot, 2, view))
+                        act(self.copy(at, slot, 2, view, sem=FORWARD[mask] + 1))
 
                 if mask == YN:
 
                     @pl.when(x_way == 0)
                     def _():
-                        act(self.copy(at, slot, 1, view))
+                        act(self.copy(at, slot, 1, view, sem=FORWARD[mask] + 1))
 
             self.pieces(at, t, body)
 
@@ -205,11 +206,11 @@
                 self.copy(at, slot, 0, view).wait_recv()
             for slot, view in views:
                 if mask in (XN, YN, DIAG):
-                    self.copy(at, slot, 0, view).start()
+                    self.copy(at, slot, 0, view, sem=FORWARD[mask]).start()
                 if mask == XN and t in (0, 2):
-                    self.copy(at, slot, 2, view).start()
+                    self.copy(at, slot, 2, view, sem=FORWARD[mask] + 1).start()
                 if mask == YN and t not in (0, 2):
-                    self.copy(at, slot, 1, view).start()
+                    self.copy(at, slot, 1, view, sem=FORWARD[mask] + 1).start()
             if t == 3:
                 block = buf.at[self.buf_id, at[1], at[2]]
                 block[mid:, :mid] = block[:mid, mid:].T
@@ -236,11 +237,12 @@
             self.each(far, lambda k, at, t: self.forward_any(k, far, at, t, lambda copy: copy.wait_send()))
 
     def part_copy(rnd, src, mask):
+        rnd = jnp.int32(rnd)
         return pltpu.make_async_remote_copy(
             src_ref=parts.at[rnd, src],
             dst_ref=parts.at[rnd, src],
             send_sem=part_send.at[mask],
-            recv_sem=part_recv.at[rnd, src],
+            recv_sem=part_recv.at[part(rnd), src],
             device_id=devices[mask],
             device_id_type=MESH,
         )
@@ -634,10 +636,10 @@
                 pltpu.VMEM((STEPS + 2, PANELS, 8, 128), f32),
                 pltpu.VMEM((8, blk_n), f32),
                 pltpu.VMEM((3, 8, 128), f32),
-                pltpu.SemaphoreType.DMA((PANELS, SLOTS + CORNERS, 3)),
+                pltpu.SemaphoreType.DMA((8, SLOTS + CORNERS)),
                 pltpu.SemaphoreType.DMA((PANELS, SLOTS + CORNERS)),
                 pltpu.SemaphoreType.DMA((PANELS,)),
-                pltpu.SemaphoreType.DMA((STEPS + 2, PANELS)),
+                pltpu.SemaphoreType.DMA((2, PANELS)),
                 pltpu.SemaphoreType.DMA((PANELS,)),
                 pltpu.SemaphoreType.DMA((PANELS,)),
             ],

time: 206 us -> 205 us (level)
  no operation moved by 1% of the time
where the time goes in v9:
time: 205 us
  Pallas kernels  198 us (97%)
  local copies, waits for them, and re-layouts  3.56 us (2%)
  between operations  3.06 us (1%)
    pallas_call x1, Pallas kernels, local_fn(): pl.pallas_call(lambda *refs: kernel(n, *refs), out_shape=(jax.ShapeDtypeS...  198 us

profile of v9, /device:TPU:0, one launch (start us, length us, event | category | flops | bytes accessed | tf_op | source)
XLA Modules:
  0.0 204.6 jit_solution(18376329840131830133)
XLA Ops:
  1.3 0.0 copy-start
  1.3 1.6 copy-done
  2.9 0.0 copy-start.1
  2.9 0.7 copy-done.1
  3.5 197.9 %purify.1 = (f32[1024,512]{1,0:T(8,128)S(1)}, f32[1]{0:T(128)}) custom-call(f32[2]{0:T(128)S(1)} %copy-done.1, s32[1]{0:T(128)S(6)} %copy.7.refs_1_, f32[1024,512]{1,0:T(8,128)S(1)} %copy-done), custom_call_target="tpu_custom_call" | custom-call | tf_op jit(solution)/shard_map/purify/pallas_call | solution.py:620
  201.5 1.3 copy.8
Async XLA Ops:
  1.3 1.6 copy-start
  2.9 0.7 copy-start.1
